TPU v7x, 32 devices: a whole 2x2x4 slice. The times are simulated.
32 devices in a mesh: ens: 2 (over x), part: 4 (over z), feat: 4 (over y, core).
Axes of the slice: x: 2, y: 2, z: 4, core: 2. Of those that a mesh axis runs over, the one named last changes fastest.
Arguments:
- particles: float32 [4096, 12288], P(('ens', 'part'), 'feat'), parts along dimension 0
- prec_diag: float32 [24576], P(('ens', 'feat')), parts along dimension 0
- target_mean: float32 [24576], P(('ens', 'feat')), parts along dimension 0
- low_factor: bfloat16 [24576, 64], P(('ens', 'feat')), parts along dimension 0
Outputs:
- output: float32 [4096, 12288], P(('ens', 'part'), 'feat'), parts along dimension 0
There are 2 independent parts. A program takes and returns all parts, laid end to end along the dimension named above; each array names one.
All inputs are finite; a program needn't handle non-finite values.
Results may differ from a plain program's by a relative error of at most 0.00351321.
Values are sent between devices in bfloat16 or wider.
A program may use at most 1 GiB of HBM per device.

v0:
```python
import math
import jax
import jax.numpy as jnp
from jax import lax
from jax.sharding import PartitionSpec as P

NUM_STEPS = 3


def solution(mesh):
    part_size = mesh.shape["part"]
    feat_size = mesh.shape["feat"]

    def local_steps(local_theta, prec_loc, mean_loc, factor_loc):
        rows_loc, feat_loc = local_theta.shape
        n_total = rows_loc * part_size
        feat_total = feat_loc * feat_size
        kern_width = 2.0 * feat_total / math.log(n_total)
        step_size = 0.15 * n_total * feat_total / math.log(n_total)
        row_start = lax.axis_index("part") * rows_loc
        cur_theta = local_theta
        for step_idx in range(NUM_STEPS):
            x_dev = cur_theta - mean_loc[None, :]
            proj_part = jnp.dot(x_dev.astype(jnp.bfloat16), factor_loc, preferred_element_type=jnp.float32)
            proj_low = lax.psum(proj_part, "feat")
            low_term = jnp.einsum("nr,dr->nd", proj_low.astype(jnp.bfloat16), factor_loc, preferred_element_type=jnp.float32)
            grad_b = (-(x_dev * prec_loc[None, :] + low_term)).astype(jnp.bfloat16)
            theta_b = cur_theta.astype(jnp.bfloat16)
            theta_all = lax.all_gather(theta_b, "part", axis=0, tiled=True)
            gram_part = jnp.einsum("nd,md->nm", theta_b, theta_all, preferred_element_type=jnp.float32)
            sq_part = jnp.einsum("md,md->m", theta_all, theta_all, preferred_element_type=jnp.float32)
            gram_rows, sq_norm = lax.psum((gram_part, sq_part), "feat")
            sq_own = lax.dynamic_slice_in_dim(sq_norm, row_start, rows_loc)
            sq_dist = jnp.maximum(sq_own[:, None] + sq_norm[None, :] - 2.0 * gram_rows, 0.0)
            kern_b = jnp.exp(-sq_dist / kern_width).astype(jnp.bfloat16)
            row_mass = jnp.sum(kern_b, axis=1, dtype=jnp.float32)
            grad_all = lax.all_gather(grad_b, "part", axis=0, tiled=True)
            drive_term = jnp.dot(kern_b, grad_all, preferred_element_type=jnp.float32)
            pull_term = jnp.dot(kern_b, theta_all, preferred_element_type=jnp.float32)
            update_dir = (drive_term + (2.0 / kern_width) * (row_mass[:, None] * theta_b.astype(jnp.float32) - pull_term)) / n_total
            cur_theta = cur_theta + step_size * update_dir
        return cur_theta

    row_spec = P(("ens", "part"), "feat")
    vec_spec = P(("ens", "feat"))
    fac_spec = P(("ens", "feat"), None)
    return jax.shard_map(local_steps, mesh=mesh, in_specs=(row_spec, vec_spec, vec_spec, fac_spec), out_specs=row_spec, check_vma=False)
```

profile of v0, /device:TPU:0, one launch (start us, length us, event | category | flops | bytes accessed | tf_op | source)
XLA Modules:
  0.0 1714.8 jit_solution(14697734620099831370)
XLA Ops:
  6.5 5.0 convert_element_type.63
  11.5 0.0 all-reduce.10.cloned.1.call-start
  11.6 221.5 %all-gather.7.cloned.1.call-done = bf16[2048,3072]{1,0:T(8,128)(2,1)} async-done(((bf16[512,3072]{1,0:T(8,128)(2,1)}), bf16[2048,3072]{1,0:T(8,128)(2,1)}) %all-gather.7.cloned.1.call-update) | async-done | bytes 12582928 | tf_op jit(solution)/shard_map/all_gather | solution.py:29
  233.1 13.8 fusion.14
  246.9 0.0 all-gather.9.cloned.1.call-start
  247.0 3.7 fusion.3
  250.7 7.1 fusion.2
  257.8 20.7 %all-reduce.15 = (f32[2048]{0:T(1024)S(1)}, bf16[512,64]{1,0:T(8,128)(2,1)S(1)}) all-reduce(f32[2048]{0:T(1024)S(1)} %fusion.2, f32[512,64]{1,0:T(8,128)S(1)} %fusion.3), channel_id=1, replica_groups=mesh['ens'=2,'part'=4,'feat'=4] {'feat'}, use_global_device_ids=true, to_apply=%region_0.0 | all-reduce | flops 34816 | bytes 212992 | tf_op jit(solution)/shard_map/psum | solution.py:32
  278.5 5.5 negate_convert_fusion.2
  284.0 0.0 all-gather.9.cloned.1.call-update
  284.0 0.2 all-gather.11.cloned.1.call-start
  284.3 0.1 dynamic_slice.9
  284.4 50.7 %all-reduce.10.cloned.1.call-done = f32[512,2048]{1,0:T(8,128)} async-done(((f32[512,2048]{1,0:T(8,128)}), f32[512,2048]{1,0:T(8,128)}) %all-reduce.10.cloned.1.call-update) | async-done | bytes 4194320 | tf_op jit(solution)/shard_map/psum | solution.py:32
  335.0 4.9 convert_reduce_fusion.2
  339.9 215.5 %all-gather.9.cloned.1.call-done = bf16[2048,3072]{1,0:T(8,128)(2,1)} async-done(((bf16[512,3072]{1,0:T(8,128)(2,1)}), bf16[2048,3072]{1,0:T(8,128)(2,1)}) %all-gather.9.cloned.1.call-update) | async-done | bytes 12582928 | tf_op jit(solution)/shard_map/all_gather | solution.py:37
  555.4 10.1 fusion.16
  565.6 12.6 fusion.12
  578.2 0.0 all-reduce.12.cloned.1.call-start
  578.2 217.0 %all-gather.11.cloned.1.call-done = bf16[2048,3072]{1,0:T(8,128)(2,1)} async-done(((bf16[512,3072]{1,0:T(8,128)(2,1)}), bf16[2048,3072]{1,0:T(8,128)(2,1)}) %all-gather.11.cloned.1.call-update) | async-done | bytes 12582928 | tf_op jit(solution)/shard_map/all_gather | solution.py:29
  795.2 11.9 fusion.17
  807.1 0.0 all-reduce.12.cloned.1.call-update
  807.2 0.3 all-gather.13.cloned.1.call-start
  807.4 3.7 fusion.4
  811.2 7.1 fusion.1
  818.3 20.6 %all-reduce.16 = (f32[2048]{0:T(1024)S(1)}, bf16[512,64]{1,0:T(8,128)(2,1)S(1)}) all-reduce(f32[2048]{0:T(1024)S(1)} %fusion.1, f32[512,64]{1,0:T(8,128)S(1)} %fusion.4), channel_id=1, replica_groups=mesh['ens'=2,'part'=4,'feat'=4] {'feat'}, use_global_device_ids=true, to_apply=%region_4.0 | all-reduce | flops 34816 | bytes 212992 | tf_op jit(solution)/shard_map/psum | solution.py:32
  838.9 5.5 negate_convert_fusion.1
  844.5 0.0 all-gather.15.cloned.1.call-start
  844.5 0.1 dynamic_slice.10
  844.6 50.7 %all-reduce.12.cloned.1.call-done = f32[512,2048]{1,0:T(8,128)} async-done(((f32[512,2048]{1,0:T(8,128)}), f32[512,2048]{1,0:T(8,128)}) %all-reduce.12.cloned.1.call-update) | async-done | bytes 4194320 | tf_op jit(solution)/shard_map/psum | solution.py:32
  895.3 4.9 convert_reduce_fusion.1
  900.1 215.4 %all-gather.13.cloned.1.call-done = bf16[2048,3072]{1,0:T(8,128)(2,1)} async-done(((bf16[512,3072]{1,0:T(8,128)(2,1)}), bf16[2048,3072]{1,0:T(8,128)(2,1)}) %all-gather.13.cloned.1.call-update) | async-done | bytes 12582928 | tf_op jit(solution)/shard_map/all_gather | solution.py:37
  1115.5 12.1 fusion.18
  1127.7 15.4 fusion.13
  1143.1 0.0 all-gather.15.cloned.1.call-update
  1143.1 0.3 all-reduce.14.cloned.1.call-start
  1143.4 216.7 %all-gather.15.cloned.1.call-done = bf16[2048,3072]{1,0:T(8,128)(2,1)} async-done(((bf16[512,3072]{1,0:T(8,128)(2,1)}), bf16[2048,3072]{1,0:T(8,128)(2,1)}) %all-gather.15.cloned.1.call-update) | async-done | bytes 12582928 | tf_op jit(solution)/shard_map/all_gather | solution.py:29
  1360.1 11.9 fusion.19
  1372.1 0.0 all-gather.17.cloned.1.call-start
  1372.1 3.7 fusion.5
  1375.9 7.1 fusion
  1383.0 20.9 %all-reduce.17 = (f32[2048]{0:T(1024)S(1)}, bf16[512,64]{1,0:T(8,128)(2,1)S(1)}) all-reduce(f32[2048]{0:T(1024)S(1)} %fusion, f32[512,64]{1,0:T(8,128)S(1)} %fusion.5), channel_id=1, replica_groups=mesh['ens'=2,'part'=4,'feat'=4] {'feat'}, use_global_device_ids=true, to_apply=%region_8.0 | all-reduce | flops 34816 | bytes 212992 | tf_op jit(solution)/shard_map/psum | solution.py:32
  1403.9 5.5 negate_convert_fusion
  1409.5 0.1 dynamic_slice.11
  1409.6 50.6 %all-reduce.14.cloned.1.call-done = f32[512,2048]{1,0:T(8,128)} async-done(((f32[512,2048]{1,0:T(8,128)}), f32[512,2048]{1,0:T(8,128)}) %all-reduce.14.cloned.1.call-update) | async-done | bytes 4194320 | tf_op jit(solution)/shard_map/psum | solution.py:32
  1460.2 4.9 convert_reduce_fusion
  1465.1 215.5 %all-gather.17.cloned.1.call-done = bf16[2048,3072]{1,0:T(8,128)(2,1)} async-done(((bf16[512,3072]{1,0:T(8,128)(2,1)}), bf16[2048,3072]{1,0:T(8,128)(2,1)}) %all-gather.17.cloned.1.call-update) | async-done | bytes 12582928 | tf_op jit(solution)/shard_map/all_gather | solution.py:37
  1680.6 12.1 fusion.20
  1692.8 15.0 multiply_add_fusion
  (38 shorter events, 0.2 us)
Async XLA Ops:
  6.5 240.4 %copy-start = (bf16[3072,64]{0,1:T(8,128)(2,1)S(1)}, bf16[3072,64]{0,1:T(8,128)(2,1)}, u32[]{:S(2)}) copy-start(bf16[3072,64]{0,1:T(8,128)(2,1)} %param.7) | copy-start | bytes 1179652
  6.5 226.6 %all-gather.7.cloned.1.call-start = ((), (), s32[]{:S(2)}) async-start(), calls=%async_computation | async-start | bytes 15728640 | tf_op jit(solution)/shard_map/all_gather | solution.py:29
  11.5 235.4 %copy-start.6 = (f32[3072]{0:T(1024)S(1)}, f32[3072]{0:T(1024)}, u32[]{:S(2)}) copy-start(f32[3072]{0:T(1024)} %param.6) | copy-start | bytes 36868
  11.5 323.5 %all-reduce.10.cloned.1.call-start = ((), (), s32[]{:S(2)}) async-start(), calls=%async_computation.1 | async-start | bytes 8388608 | tf_op jit(solution)/shard_map/psum | solution.py:32
  246.9 308.5 %all-gather.9.cloned.1.call-start = ((), (), s32[]{:S(2)}) async-start(), calls=%async_computation.2 | async-start | bytes 15728640 | tf_op jit(solution)/shard_map/all_gather | solution.py:37
  250.7 27.8 %copy-start.7 = (f32[3072]{0:T(1024)S(1)}, f32[3072]{0:T(1024)}, u32[]{:S(2)}) copy-start(f32[3072]{0:T(1024)} %param.5) | copy-start | bytes 36868
  284.0 511.1 %all-gather.11.cloned.1.call-start = ((), (), s32[]{:S(2)}) async-start(), calls=%async_computation.3 | async-start | bytes 15728640 | tf_op jit(solution)/shard_map/all_gather | solution.py:29
  335.0 230.5 %slice-start = ((s8[6291456]{0:T(1024)(128)(4,1)}), s8[2097152]{0:T(1024)(128)(4,1)S(1)}, s32[]{:S(2)}) async-start(s8[6291456]{0:T(1024)(128)(4,1)} %bitcast.26), calls=%async_computation.9 | async-start | bytes 4194304
  555.4 10.1 slice-start.1
  555.4 10.2 copy-start.4
  578.2 317.1 %all-reduce.12.cloned.1.call-start = ((), (), s32[]{:S(2)}) async-start(), calls=%async_computation.4 | async-start | bytes 8388608 | tf_op jit(solution)/shard_map/psum | solution.py:32
  807.2 308.4 %all-gather.13.cloned.1.call-start = ((), (), s32[]{:S(2)}) async-start(), calls=%async_computation.5 | async-start | bytes 15728640 | tf_op jit(solution)/shard_map/all_gather | solution.py:37
  844.5 515.7 %all-gather.15.cloned.1.call-start = ((), (), s32[]{:S(2)}) async-start(), calls=%async_computation.6 | async-start | bytes 15728640 | tf_op jit(solution)/shard_map/all_gather | solution.py:29
  895.3 232.4 %slice-start.2 = ((s8[6291456]{0:T(1024)(128)(4,1)}), s8[2097152]{0:T(1024)(128)(4,1)S(1)}, s32[]{:S(2)}) async-start(s8[6291456]{0:T(1024)(128)(4,1)} %bitcast.28), calls=%async_computation.11 | async-start | bytes 4194304
  1115.5 12.1 slice-start.3
  1115.5 12.1 copy-start.1
  1115.5 12.1 copy-start.3
  1143.1 317.1 %all-reduce.14.cloned.1.call-start = ((), (), s32[]{:S(2)}) async-start(), calls=%async_computation.7 | async-start | bytes 8388608 | tf_op jit(solution)/shard_map/psum | solution.py:32
  1372.1 308.5 %all-gather.17.cloned.1.call-start = ((), (), s32[]{:S(2)}) async-start(), calls=%async_computation.8 | async-start | bytes 15728640 | tf_op jit(solution)/shard_map/all_gather | solution.py:37
  1460.2 232.5 %slice-start.4 = ((s8[6291456]{0:T(1024)(128)(4,1)}), s8[2097152]{0:T(1024)(128)(4,1)S(1)}, s32[]{:S(2)}) async-start(s8[6291456]{0:T(1024)(128)(4,1)} %bitcast.30), calls=%async_computation.13 | async-start | bytes 4194304
  1680.6 12.1 slice-start.5
  1680.6 12.1 copy-start.2
  1680.6 12.1 copy-start.5
Sparse Core Ops, SparseCore 0:
  11.7 221.4 all-gather.6
  247.0 87.9 all-reduce.9
  336.6 218.7 all-gather.8
  578.3 216.8 all-gather.10
  807.3 87.9 all-reduce.11
  896.7 218.7 all-gather.12
  1143.3 216.8 all-gather.14
  1372.2 87.9 all-reduce.13
  1461.8 218.7 all-gather.16
where the time goes:
time: 1720 us; the launch traced here: 1710 us
  waiting for transfers between devices  1450 us (84%)
  matrix products  143 us (8%)
  blocking collectives  62.2 us (4%)
  other arithmetic  40.8 us (2%)
    all_gather x3, waiting for transfers between devices, local_steps(): theta_all = lax.all_gather(theta_b, 'part', axis=0, tiled=True)  655 us
    all_gather x3, waiting for transfers between devices, local_steps(): grad_all = lax.all_gather(grad_b, 'part', axis=0, tiled=True)  646 us
    psum x3, waiting for transfers between devices, local_steps(): gram_rows, sq_norm = lax.psum((gram_part, sq_part), 'feat')  152 us
    psum x3, blocking collectives, local_steps(): gram_rows, sq_norm = lax.psum((gram_part, sq_part), 'feat')  62.2 us
    dot_general x3, matrix products, local_steps(): pull_term = jnp.dot(kern_b, theta_all, preferred_element_type=jnp.float32)  43 us
    dot_general x3, matrix products, local_steps(): jnp.einsum('nd,md->nm', theta_b, theta_all, preferred_element_type=jnp.fl...  37.6 us
  transfers between devices with their start and end apart: 9, of which 9 were waited for; matrix products, arithmetic and copies ran while one was open for 4% of the time, Pallas kernels for 0%

commit v1 on v0

v1 whole, which is shorter than its diff:
```python
import math
import jax
import jax.numpy as jnp
from jax import lax
from jax.experimental import pallas as pl
from jax.experimental.pallas import tpu as pltpu
from jax.sharding import PartitionSpec as P

NUM_STEPS = 3
BLK = 128
SPAN = 9
PW = (SPAN + 1) * BLK
GW = SPAN * BLK
NCH = 4
CH = BLK // NCH
TILE = 256
BF = jnp.bfloat16
F32 = jnp.float32
MESH = pl.DeviceIdType.MESH
NT = (((1,), (1,)), ((), ()))


def _dot(a, b):
    return jnp.dot(a, b, preferred_element_type=F32)


def _dot_nt(a, b):
    return lax.dot_general(a, b, NT, preferred_element_type=F32)


def _kernel(n_total, kern_width, step_size,
            theta_in, prec_ref, mean_ref, u0_ref, u1_ref, out_ref,
            th, tb, tsib, ab, gp, fr, cr, zr, kp, k2, zown, zsnd, zrcv, sfull,
            in_s, in_r, tx_s, tx_r, zx_s, zx_r, fy_s, fy_r, ch_s, ch_r, zy_s, zy_r,
            kc_s, kc_r, ky_s, ky_r, kx_s, kx_r, out_s, out_r):
    z = lax.axis_index("part")
    f = lax.axis_index("feat")
    y = f // 2
    c = f % 2
    width = th.shape[1]
    half = n_total // 2
    group = n_total // 4

    def dev(zz, yy, cc):
        return {"part": zz, "feat": 2 * yy + cc}

    me = dev(z, y, c)
    ynb = dev(z, 1 - y, c)
    sib = dev(z, y, 1 - c)
    is_end = jnp.logical_or(z == 0, z == 3)
    is_mid = jnp.logical_not(is_end)
    e1 = jnp.where(z < 2, 1, 0)
    e2 = 1 - e1

    def toward(e):
        return dev(jnp.clip(z + 2 * e - 1, 0, 3), y, c)

    def away(e):
        return dev(jnp.clip(z - 2 * e + 1, 0, 3), y, c)

    def rc(src, dst, ss, rs, d):
        return pltpu.make_async_remote_copy(src_ref=src, dst_ref=dst, send_sem=ss, recv_sem=rs,
                                            device_id=d, device_id_type=MESH)

    bar = pltpu.get_barrier_semaphore()
    for k in range(1, 4):
        pl.semaphore_signal(bar, inc=1, device_id=dev((z + k) % 4, y, c), device_id_type=MESH)
    pl.semaphore_signal(bar, inc=1, device_id=ynb, device_id_type=MESH)
    pl.semaphore_signal(bar, inc=1, device_id=sib, device_id_type=MESH)
    pl.semaphore_wait(bar, 5)

    def grp(zz):
        return pl.multiple_of(((zz + 4 - 2 * c) % 4) * group, group)

    def in_copy(zz):
        return rc(theta_in.at[:, pl.ds(pl.multiple_of(zz * width, BLK), width)], th.at[pl.ds(grp(z), group), :],
                  in_s.at[zz], in_r.at[z], dev(zz, y, c))

    def in_local():
        return pltpu.make_async_copy(theta_in.at[:, pl.ds(pl.multiple_of(z * width, BLK), width)],
                                     th.at[pl.ds(grp(z), group), :], in_r.at[z])

    in_local().start()
    for dist in (3, 2, 1):
        for zz in (z + dist, z - dist):
            @pl.when(jnp.logical_and(zz >= 0, zz < 4))
            def _(zz=zz):
                in_copy(zz).start()

    def t_copy(par, i):
        src = tb.at[par, pl.ds(pl.multiple_of(i * TILE, TILE), TILE), :]
        dst = tsib.at[pl.ds(pl.multiple_of(((i + 4) % 8) * TILE, TILE), TILE), :]
        return rc(src, dst, tx_s.at[i], tx_r.at[(i + 4) % 8], sib)

    def z_copy():
        return rc(zsnd, zrcv, zx_s, zx_r, sib)

    eye = (lax.broadcasted_iota(jnp.int32, (BLK, BLK), 0) == lax.broadcasted_iota(jnp.int32, (BLK, BLK), 1))

    def finish_rows(i, par):
        rows = pl.ds(pl.multiple_of(i * TILE, TILE), TILE)
        tt = th[rows, :].astype(BF)
        tb[par, rows, :] = tt
        t_copy(par, i).start()
        for s in range(TILE // BLK):
            b = i * (TILE // BLK) + s
            t_blk = tt[s * BLK:(s + 1) * BLK].astype(F32)
            s_col = jnp.sum(t_blk * t_blk, axis=1, keepdims=True)
            s_row = jnp.sum(jnp.where(eye, jnp.broadcast_to(s_col, (BLK, BLK)), 0.0), axis=0, keepdims=True)
            zsnd[8, pl.ds(b, 1), :] = s_row
            x_blk = (th[pl.ds(pl.multiple_of(b * BLK, BLK), BLK), :] - mean_ref[...]).astype(BF)
            zq = _dot(x_blk[:BLK // 2], u0_ref[...]) + _dot(x_blk[BLK // 2:], u1_ref[...])

            @pl.when(b < 8)
            def _():
                zown[b] = zq

            @pl.when(b >= 8)
            def _():
                zsnd[b - 8] = zq

    def first_rows(k, carry):
        zz = (z + k) % 4

        @pl.when(k == 0)
        def _():
            in_local().wait()

        @pl.when(k > 0)
        def _():
            rc(th.at[pl.ds(grp(zz), group), :], th.at[pl.ds(grp(zz), group), :], in_s.at[zz], in_r.at[zz], me).wait_recv()
        for s in range(group // TILE):
            finish_rows(((zz + 4 - 2 * c) % 4) * (group // TILE) + s, 0)
        return carry

    lax.fori_loop(0, 4, first_rows, 0)
    z_copy().start()
    for k in range(1, 4):
        in_copy((z + k) % 4).wait_send()

    def qf(yy, e):
        return yy * 2 + e

    def qz(yy, e):
        return 4 + yy * 2 + e

    def crow(i):
        return pl.ds(i * CH, CH)

    def fy_copy(e, i):
        return rc(gp.at[qf(1 - y, e), crow(i), :], fr.at[e, crow(i), :], fy_s.at[e, i], fy_r.at[e, i], ynb)

    def chain_q(n, e):
        return (qz(1 - y, e), qz(y, e), qf(y, e))[n // NCH]

    def chain_copy(n, e):
        return rc(gp.at[chain_q(n, e), crow(n % NCH), :], cr.at[e, n], ch_s.at[e, n], ch_r.at[e, n], toward(e))

    def zy_copy(i):
        return rc(gp.at[qz(1 - y, e2), crow(i), :], zr.at[crow(i), :], zy_s.at[i], zy_r.at[i], ynb)

    HR = BLK // 2

    def krow(ch):
        return pl.ds(ch * HR, HR)

    def kc_copy(e, j, ch, q):
        return rc(kp.at[0, q, krow(ch), :], kp.at[0, q, krow(ch), :], kc_s.at[e, j * 2 + ch], kc_r.at[e, j * 2 + ch], away(e))

    def ky_copy(e, kind, ch, q):
        return rc(kp.at[0, q, krow(ch), :], kp.at[0, q, krow(ch), :], ky_s.at[e, kind, ch], ky_r.at[e, kind, ch], ynb)

    def kx_copy(ch, q):
        return rc(kp.at[0, q, krow(ch), :], kp.at[1, q, krow(ch), :], kx_s.at[q, ch], kx_r.at[q, ch], sib)

    def step(t, carry):
        par = t % 2

        def t_wait(i, cc):
            t_copy(par, i).wait()
            return cc

        lax.fori_loop(0, 8, t_wait, 0)
        z_copy().wait()
        sfull[0:8, :] = zsnd[8, 0:8, :] + zrcv[8, 8:16, :]
        sfull[8:16, :] = zsnd[8, 8:16, :] + zrcv[8, 0:8, :]

        def panel(q):
            rows = pl.ds(pl.multiple_of(q * BLK, BLK), BLK)
            win = pl.ds(pl.multiple_of(q * BLK, BLK), GW)
            gp[q, :, 0:GW] = _dot_nt(tb[par, rows, :], tb[par, win, :]) + _dot_nt(tsib[rows, :], tsib[win, :])
            gp[q, 0:16, GW:PW] = sfull[...]
            gp[q, 16:80, GW:PW] = zown[q] + zrcv[q]
            gp[q, 80:BLK, GW:PW] = jnp.zeros((BLK - 80, BLK), F32)

        def mk_panels(m, cc):
            e = jnp.where(m % 2 == 0, e1, e2)
            g = m // 2
            q = jnp.where(g == 0, qf(1 - y, e), jnp.where(g == 1, qz(1 - y, e), jnp.where(g == 2, qz(y, e), qf(y, e))))
            panel(q)

            @pl.when(g == 0)
            def _():
                for i in range(NCH):
                    fy_copy(e, i).start()

            for gg in (1, 2):
                @pl.when(jnp.logical_and(is_end, m == 2 * gg))
                def _(gg=gg):
                    for i in range(NCH):
                        chain_copy((gg - 1) * NCH + i, e1).start()
            return cc

        lax.fori_loop(0, 8, mk_panels, 0)

        def kern_panel(q):
            s_col = jnp.sum(jnp.where(eye, jnp.broadcast_to(sfull[pl.ds(q, 1), :], (BLK, BLK)), 0.0), axis=1, keepdims=True)
            for k in range(SPAN):
                cols = slice(k * BLK, (k + 1) * BLK)
                dist = jnp.maximum(s_col + sfull[pl.ds(q + k, 1), :] - 2.0 * gp[q, :, cols], 0.0)
                kp[0, q, :, cols] = jnp.exp(dist * (-1.0 / kern_width)).astype(BF)
            kp[0, q, 0:HR, GW:PW] = jnp.zeros((HR, BLK), BF)
            kp[0, q, HR:BLK, GW:PW] = gp[q, 16:80, GW:PW].astype(BF)

        def send_own(j, q):
            for ch in range(2):
                kc_copy(e2, j, ch, q).start()
                ky_copy(e2, 1 - j, ch, q).start()
                kx_copy(ch, q).start()

        for n in range(3 * NCH):
            i = n % NCH
            rows = crow(i)

            def take(e, with_chain, with_y):
                q = chain_q(n, e)
                val = gp[q, rows, :]
                if with_y:
                    fy_copy_in = rc(fr.at[e, rows, :], fr.at[e, rows, :], fy_s.at[e, i], fy_r.at[e, i], ynb)
                    fy_copy_in.wait_recv()
                    val = val + fr[e, rows, :]
                if with_chain:
                    rc(cr.at[e, n], cr.at[e, n], ch_s.at[e, n], ch_r.at[e, n], me).wait_recv()
                    val = val + cr[e, n]
                gp[q, rows, :] = val

            @pl.when(is_mid)
            def _(n=n, take=take):
                for e in (e1, e2):
                    take(e, True, n >= 2 * NCH)
                    chain_copy(n, e).start()

            @pl.when(is_end)
            def _(n=n, i=i, take=take, rows=rows):
                if n >= 2 * NCH:
                    take(e1, False, True)
                    chain_copy(n, e1).start()
                take(e2, True, n >= 2 * NCH)
                if n < NCH:
                    zy_copy(i).start()
                elif n < 2 * NCH:
                    rc(zr.at[rows, :], zr.at[rows, :], zy_s.at[i], zy_r.at[i], me).wait_recv()
                    q = qz(y, e2)
                    gp[q, rows, :] = gp[q, rows, :] + zr[rows, :]
                if n == 2 * NCH - 1:
                    q = qz(y, e2)
                    sfull[...] = gp[q, 0:16, GW:PW]
                    kern_panel(q)
                    send_own(0, q)
                if n == 3 * NCH - 1:
                    q = qf(y, e2)
                    kern_panel(q)
                    send_own(1, q)

        def assemble(h, q):
            lo = pl.ds(pl.multiple_of(q * BLK, BLK), BLK)
            for k in range(SPAN):
                blk = kp[h, q, :, k * BLK:(k + 1) * BLK]
                k2[h, lo, pl.ds(pl.multiple_of((q + k) * BLK, BLK), BLK)] = blk
                if 1 <= k <= 7:
                    flip = (q + k) // 8
                    k2[(h + flip) % 2, pl.ds(pl.multiple_of((q + k - 8 * flip) * BLK, BLK), BLK),
                       pl.ds(pl.multiple_of((q + 8 * flip) * BLK, BLK), BLK)] = blk.T
            zb = kp[h, q, HR:BLK, GW:PW]
            for s, u_ref in ((0, u0_ref), (1, u1_ref)):
                rows = pl.ds(pl.multiple_of((h * 8 + q) * BLK + s * HR, HR), HR)
                low = _dot_nt(zb, u_ref[...])
                x_dev = th[rows, :] - mean_ref[...]
                ab[rows, :] = (-(x_dev * prec_ref[...] + low)).astype(BF)

        def slot_q(slot):
            j = slot // 2
            e = jnp.where(slot % 2 == 0, e2, e1)
            q = jnp.where(j == 0, qz(y, e), jnp.where(j == 1, qf(y, e), jnp.where(j == 2, qz(1 - y, e), qf(1 - y, e))))
            return j, e, q

        def slot_body(slot, cc):
            @pl.when(slot < 8)
            def _():
                j, e, q = slot_q(slot)
                at_origin = jnp.logical_and(is_end, e == e2)
                own = jnp.logical_and(at_origin, j < 2)
                from_y = jnp.logical_or(j == 3, jnp.logical_and(at_origin, j == 2))
                from_chain = jnp.logical_not(jnp.logical_or(own, from_y))
                last = jnp.logical_and(is_end, e == e1)
                fwd = jnp.logical_and(jnp.logical_and(j < 3, jnp.logical_not(last)), jnp.logical_not(own))
                kind = jnp.where(j == 3, 0, 1)
                for ch in range(2):
                    buf = kp.at[0, q, krow(ch), :]

                    @pl.when(from_chain)
                    def _():
                        jj = jnp.minimum(j, 2)
                        rc(buf, buf, kc_s.at[e, jj * 2 + ch], kc_r.at[e, jj * 2 + ch], me).wait_recv()

                    @pl.when(from_y)
                    def _():
                        rc(buf, buf, ky_s.at[e, kind, ch], ky_r.at[e, kind, ch], me).wait_recv()

                    @pl.when(fwd)
                    def _():
                        kc_copy(e, j, ch, q).start()

                    @pl.when(jnp.logical_and(j == 1, jnp.logical_not(own)))
                    def _():
                        ky_copy(e, 0, ch, q).start()

                    @pl.when(jnp.logical_not(own))
                    def _():
                        kx_copy(ch, q).start()
                assemble(0, q)

            @pl.when(slot > 0)
            def _():
                _, _, q = slot_q(slot - 1)
                for ch in range(2):
                    buf = kp.at[1, q, krow(ch), :]
                    rc(buf, buf, kx_s.at[q, ch], kx_r.at[q, ch], me).wait_recv()
                assemble(1, q)
            return cc

        lax.fori_loop(0, 9, slot_body, 0)

        for e in range(2):
            for i in range(NCH):
                fy_copy(e, i).wait_send()
        for n in range(3 * NCH):
            chain_copy(n, e1).wait_send()

            @pl.when(is_mid)
            def _(n=n):
                chain_copy(n, e2).wait_send()

        @pl.when(is_end)
        def _():
            for i in range(NCH):
                zy_copy(i).wait_send()

        def phi_tile(i, cc):
            h = i // 4
            rows = pl.ds(pl.multiple_of(i * TILE, TILE), TILE)
            krows = pl.ds(pl.multiple_of((i % 4) * TILE, TILE), TILE)
            first = pl.ds(pl.multiple_of(h * half, half), half)
            second = pl.ds(pl.multiple_of((1 - h) * half, half), half)
            ka = k2[h, krows, 0:half]
            kb = k2[h, krows, half:n_total]
            drive = _dot(ka, ab[first, :]) + _dot(kb, ab[second, :])
            pull = _dot(ka, tb[par, first, :]) + _dot(kb, tb[par, second, :])
            mass = jnp.sum(ka.astype(F32), axis=1, keepdims=True) + jnp.sum(kb.astype(F32), axis=1, keepdims=True)
            t_own = tb[par, rows, :].astype(F32)
            upd = (drive + (2.0 / kern_width) * (mass * t_own - pull)) * (1.0 / n_total)
            th[rows, :] = th[rows, :] + step_size * upd

            @pl.when(t < NUM_STEPS - 1)
            def _():
                finish_rows(i, 1 - par)

            @pl.when(t == NUM_STEPS - 1)
            def _():
                zz = (i // 2 + 2 * c) % 4
                dst = out_ref.at[pl.ds(pl.multiple_of((i % 2) * TILE, TILE), TILE), pl.ds(pl.multiple_of(z * width, BLK), width)]

                @pl.when(zz == z)
                def _():
                    pltpu.make_async_copy(th.at[rows, :], dst, out_s.at[i]).start()

                @pl.when(zz != z)
                def _():
                    rc(th.at[rows, :], dst, out_s.at[i], out_r.at[z, i % 2], dev(zz, y, c)).start()
            return cc

        lax.fori_loop(0, 8, phi_tile, 0)

        @pl.when(t < NUM_STEPS - 1)
        def _():
            z_copy().start()

        for ch in range(2):
            for e in range(2):
                ky_copy(e, 0, ch, qf(y, e)).wait_send()

            @pl.when(is_end)
            def _(ch=ch):
                ky_copy(e2, 1, ch, qz(y, e2)).wait_send()
            for j in range(3):
                q2 = (qz(y, e2), qf(y, e2), qz(1 - y, e2))[j]
                q1 = (qz(y, e1), qf(y, e1), qz(1 - y, e1))[j]
                kc_copy(e2, j, ch, q2).wait_send()

                @pl.when(is_mid)
                def _(ch=ch, j=j, q1=q1):
                    kc_copy(e1, j, ch, q1).wait_send()
            for q in range(8):
                kx_copy(ch, q).wait_send()
        return carry

    lax.fori_loop(0, NUM_STEPS, step, 0)

    def out_wait(i, cc):
        zz = (i // 2 + 2 * c) % 4
        rows = pl.ds(pl.multiple_of(i * TILE, TILE), TILE)
        dst = out_ref.at[pl.ds(pl.multiple_of((i % 2) * TILE, TILE), TILE), pl.ds(pl.multiple_of(z * width, BLK), width)]

        @pl.when(zz == z)
        def _():
            pltpu.make_async_copy(th.at[rows, :], dst, out_s.at[i]).wait()

        @pl.when(zz != z)
        def _():
            rc(th.at[rows, :], dst, out_s.at[i], out_r.at[z, i % 2], dev(zz, y, c)).wait_send()
        return cc

    lax.fori_loop(0, 8, out_wait, 0)
    for k in range(1, 4):
        zz = (z + k) % 4
        for s in range(2):
            dst = out_ref.at[pl.ds(s * TILE, TILE), pl.ds(pl.multiple_of(zz * width, BLK), width)]
            rc(dst, dst, out_s.at[0], out_r.at[zz, s], me).wait_recv()


def solution(mesh):
    part_size = mesh.shape["part"]
    feat_size = mesh.shape["feat"]

    def local_steps(local_theta, prec_loc, mean_loc, factor_loc):
        rows_loc, feat_loc = local_theta.shape
        n_total = rows_loc * part_size
        feat_total = feat_loc * feat_size
        width = feat_loc // part_size
        kern_width = 2.0 * feat_total / math.log(n_total)
        step_size = 0.15 * n_total * feat_total / math.log(n_total)
        start = lax.axis_index("part") * width
        prec = lax.dynamic_slice_in_dim(prec_loc, start, width)[None, :]
        mean = lax.dynamic_slice_in_dim(mean_loc, start, width)[None, :]
        factor = lax.dynamic_slice_in_dim(factor_loc, start, width)
        rank = factor.shape[1]
        u0 = jnp.pad(factor, ((0, 0), (0, BLK - rank)))
        u1 = jnp.pad(factor, ((0, 0), (BLK - rank, 0)))
        vmem = pl.BlockSpec(memory_space=pltpu.VMEM)
        anym = pl.BlockSpec(memory_space=pl.ANY)
        dma = pltpu.SemaphoreType.DMA
        body = lambda *refs: _kernel(n_total, kern_width, step_size, *refs)
        return pl.pallas_call(
            body,
            out_shape=jax.ShapeDtypeStruct((rows_loc, feat_loc), F32),
            in_specs=[anym, vmem, vmem, vmem, vmem],
            out_specs=anym,
            scratch_shapes=[
                pltpu.VMEM((n_total, width), F32),
                pltpu.VMEM((2, n_total, width), BF),
                pltpu.VMEM((n_total, width), BF),
                pltpu.VMEM((n_total, width), BF),
                pltpu.VMEM((8, BLK, PW), F32),
                pltpu.VMEM((2, BLK, PW), F32),
                pltpu.VMEM((2, 3 * NCH, CH, PW), F32),
                pltpu.VMEM((BLK, PW), F32),
                pltpu.VMEM((2, 8, BLK, PW), BF),
                pltpu.VMEM((2, n_total // 2, n_total), BF),
                pltpu.VMEM((8, BLK // 2, BLK), F32),
                pltpu.VMEM((9, BLK // 2, BLK), F32),
                pltpu.VMEM((9, BLK // 2, BLK), F32),
                pltpu.VMEM((16, BLK), F32),
                dma((4,)), dma((4,)), dma((8,)), dma((8,)), dma, dma,
                dma((2, NCH)), dma((2, NCH)), dma((2, 3 * NCH)), dma((2, 3 * NCH)), dma((NCH,)), dma((NCH,)),
                dma((2, 6)), dma((2, 6)), dma((2, 2, 2)), dma((2, 2, 2)), dma((8, 2)), dma((8, 2)),
                dma((8,)), dma((4, 2)),
            ],
            compiler_params=pltpu.CompilerParams(collective_id=0, has_side_effects=True, vmem_limit_bytes=63 * 1024 * 1024),
            name="svgd",
        )(local_theta, prec, mean, u0, u1)

    row_spec = P(("ens", "part"), "feat")
    vec_spec = P(("ens", "feat"))
    fac_spec = P(("ens", "feat"), None)
    return jax.shard_map(local_steps, mesh=mesh, in_specs=(row_spec, vec_spec, vec_spec, fac_spec), out_specs=row_spec, check_vma=False)
```

time: 1720 us -> 783 us (0.46)
  the two profiles are of different devices: /device:TPU:0 before, /device:TPU:15 now
where the time goes in v1:
time: 783 us
  Pallas kernels  772 us (99%)
  local copies, waits for them, and re-layouts  10 us (1%)
    pallas_call x1, Pallas kernels, local_steps(): pl.pallas_call(body, out_shape=jax.ShapeDtypeStruct((rows_loc, feat_loc),...  772 us

profile of v1, /device:TPU:15, one launch (start us, length us, event | category | flops | bytes accessed | tf_op | source)
XLA Modules:
  0.0 782.5 jit_solution(4482314710855766343)
XLA Ops:
  0.0 0.0 copy-start
  0.0 0.8 dynamic_slice.9
  0.8 0.6 broadcast_in_dim.6.refs_1_
  1.4 0.8 dynamic_slice.10
  2.2 0.6 broadcast_in_dim.7.refs_2_
  2.8 0.0 copy-done
  2.8 0.2 copy.6
  3.0 0.9 fusion
  3.8 772.4 %svgd.1 = f32[512,3072]{1,0:T(8,128)} custom-call(f32[512,3072]{1,0:T(8,128)} %refs_0_.1, f32[1,768]{1,0:T(1,128)} %broadcast_in_dim.6.refs_1_, f32[1,768]{1,0:T(1,128)} %broadcast_in_dim.7.refs_2_, bf16[768,128]{1,0:T(8,128)(2,1)} %get-tuple-element.6.refs_3_, bf16[768,128]{1,0:T(8,128)(2,1)} %get-tuple-element.5.refs_4_), custom_call_target="tpu_custom_call" | custom-call | tf_op jit(solution)/shard_map/svgd/pallas_call | solution.py:463
  776.3 6.2 copy.8
  (1 shorter events, 0.0 us)
Async XLA Ops:
  0.0 2.8 copy-start

commit v2 on v1

--- a/solution.py
+++ b/solution.py
@@ -11,8 +11,12 @@
 SPAN = 9
 PW = (SPAN + 1) * BLK
 GW = SPAN * BLK
-NCH = 4
+NCH = 8
 CH = BLK // NCH
+KCH = 4
+HR = BLK // 2
+KSKEW = 2
+SKEW = 3
 TILE = 256
 BF = jnp.bfloat16
 F32 = jnp.float32
@@ -159,13 +163,11 @@
     def zy_copy(i):
         return rc(gp.at[qz(1 - y, e2), crow(i), :], zr.at[crow(i), :], zy_s.at[i], zy_r.at[i], ynb)
 
-    HR = BLK // 2
-
     def krow(ch):
-        return pl.ds(ch * HR, HR)
+        return pl.ds(ch * (BLK // KCH), BLK // KCH)
 
     def kc_copy(e, j, ch, q):
-        return rc(kp.at[0, q, krow(ch), :], kp.at[0, q, krow(ch), :], kc_s.at[e, j * 2 + ch], kc_r.at[e, j * 2 + ch], away(e))
+        return rc(kp.at[0, q, krow(ch), :], kp.at[0, q, krow(ch), :], kc_s.at[e, j * KCH + ch], kc_r.at[e, j * KCH + ch], away(e))
 
     def ky_copy(e, kind, ch, q):
         return rc(kp.at[0, q, krow(ch), :], kp.at[0, q, krow(ch), :], ky_s.at[e, kind, ch], ky_r.at[e, kind, ch], ynb)
@@ -194,24 +196,32 @@
             gp[q, 80:BLK, GW:PW] = jnp.zeros((BLK - 80, BLK), F32)
 
         def mk_panels(m, cc):
-            e = jnp.where(m % 2 == 0, e1, e2)
-            g = m // 2
-            q = jnp.where(g == 0, qf(1 - y, e), jnp.where(g == 1, qz(1 - y, e), jnp.where(g == 2, qz(y, e), qf(y, e))))
-            panel(q)
-
-            @pl.when(g == 0)
+            k = jnp.where(is_end, jnp.where(m == 0, 2, jnp.where(m < 3, m - 1, 3)), m)
+            e = jnp.where(k % 2 == 0, e1, e2)
+            panel(jnp.where(k < 2, qf(1 - y, e), qz(1 - y, e)))
+
+            @pl.when(k < 2)
             def _():
                 for i in range(NCH):
                     fy_copy(e, i).start()
 
-            for gg in (1, 2):
-                @pl.when(jnp.logical_and(is_end, m == 2 * gg))
-                def _(gg=gg):
-                    for i in range(NCH):
-                        chain_copy((gg - 1) * NCH + i, e1).start()
+            @pl.when(jnp.logical_and(is_end, m == 0))
+            def _():
+                for i in range(NCH):
+                    chain_copy(i, e1).start()
             return cc
 
-        lax.fori_loop(0, 8, mk_panels, 0)
+        lax.fori_loop(0, 4, mk_panels, 0)
+
+        def late_panels(m, cc):
+            e = jnp.where(m % 2 == 0, e1, e2)
+            panel(jnp.where(m < 2, qz(y, e), qf(y, e)))
+
+            @pl.when(jnp.logical_and(is_end, m == 0))
+            def _():
+                for i in range(NCH):
+                    chain_copy(NCH + i, e1).start()
+            return cc
 
         def kern_panel(q):
             s_col = jnp.sum(jnp.where(eye, jnp.broadcast_to(sfull[pl.ds(q, 1), :], (BLK, BLK)), 0.0), axis=1, keepdims=True)
@@ -223,54 +233,65 @@
             kp[0, q, HR:BLK, GW:PW] = gp[q, 16:80, GW:PW].astype(BF)
 
         def send_own(j, q):
-            for ch in range(2):
+            for ch in range(KCH):
                 kc_copy(e2, j, ch, q).start()
                 ky_copy(e2, 1 - j, ch, q).start()
                 kx_copy(ch, q).start()
 
-        for n in range(3 * NCH):
+        def take(n, e, with_chain, with_y):
             i = n % NCH
             rows = crow(i)
-
-            def take(e, with_chain, with_y):
-                q = chain_q(n, e)
-                val = gp[q, rows, :]
-                if with_y:
-                    fy_copy_in = rc(fr.at[e, rows, :], fr.at[e, rows, :], fy_s.at[e, i], fy_r.at[e, i], ynb)
-                    fy_copy_in.wait_recv()
-                    val = val + fr[e, rows, :]
-                if with_chain:
-                    rc(cr.at[e, n], cr.at[e, n], ch_s.at[e, n], ch_r.at[e, n], me).wait_recv()
-                    val = val + cr[e, n]
-                gp[q, rows, :] = val
-
-            @pl.when(is_mid)
-            def _(n=n, take=take):
-                for e in (e1, e2):
-                    take(e, True, n >= 2 * NCH)
+            q = chain_q(n, e)
+            val = gp[q, rows, :]
+            if with_y:
+                rc(fr.at[e, rows, :], fr.at[e, rows, :], fy_s.at[e, i], fy_r.at[e, i], me).wait_recv()
+                val = val + fr[e, rows, :]
+            if with_chain:
+                rc(cr.at[e, n], cr.at[e, n], ch_s.at[e, n], ch_r.at[e, n], me).wait_recv()
+                val = val + cr[e, n]
+            gp[q, rows, :] = val
+
+        def mid_round(m):
+            for n, e in ((m, e1), (m - SKEW, e2)):
+                if 0 <= n < 3 * NCH:
+                    take(n, e, True, n >= 2 * NCH)
                     chain_copy(n, e).start()
 
-            @pl.when(is_end)
-            def _(n=n, i=i, take=take, rows=rows):
-                if n >= 2 * NCH:
-                    take(e1, False, True)
-                    chain_copy(n, e1).start()
-                take(e2, True, n >= 2 * NCH)
-                if n < NCH:
-                    zy_copy(i).start()
-                elif n < 2 * NCH:
-                    rc(zr.at[rows, :], zr.at[rows, :], zy_s.at[i], zy_r.at[i], me).wait_recv()
-                    q = qz(y, e2)
-                    gp[q, rows, :] = gp[q, rows, :] + zr[rows, :]
-                if n == 2 * NCH - 1:
-                    q = qz(y, e2)
-                    sfull[...] = gp[q, 0:16, GW:PW]
-                    kern_panel(q)
-                    send_own(0, q)
-                if n == 3 * NCH - 1:
-                    q = qf(y, e2)
-                    kern_panel(q)
-                    send_own(1, q)
+        def end_round(n):
+            i = n % NCH
+            rows = crow(i)
+            if NCH <= n < 2 * NCH:
+                take(n + NCH, e1, False, True)
+                chain_copy(n + NCH, e1).start()
+            take(n, e2, True, n >= 2 * NCH)
+            if n < NCH:
+                zy_copy(i).start()
+            elif n < 2 * NCH:
+                rc(zr.at[rows, :], zr.at[rows, :], zy_s.at[i], zy_r.at[i], me).wait_recv()
+                q = qz(y, e2)
+                gp[q, rows, :] = gp[q, rows, :] + zr[rows, :]
+            if n == 2 * NCH - 1:
+                q = qz(y, e2)
+                sfull[...] = gp[q, 0:16, GW:PW]
+                kern_panel(q)
+                send_own(0, q)
+            if n == 3 * NCH - 1:
+                q = qf(y, e2)
+                kern_panel(q)
+                send_own(1, q)
+
+        @pl.when(is_mid)
+        def _():
+            for m in range(3 * NCH + SKEW):
+                if m < 4:
+                    lax.fori_loop(m, m + 1, late_panels, 0)
+                mid_round(m)
+
+        @pl.when(is_end)
+        def _():
+            lax.fori_loop(0, 4, late_panels, 0)
+            for n in range(3 * NCH):
+                end_round(n)
 
         def assemble(h, q):
             lo = pl.ds(pl.multiple_of(q * BLK, BLK), BLK)
@@ -288,58 +309,93 @@
                 x_dev = th[rows, :] - mean_ref[...]
                 ab[rows, :] = (-(x_dev * prec_ref[...] + low)).astype(BF)
 
-        def slot_q(slot):
-            j = slot // 2
-            e = jnp.where(slot % 2 == 0, e2, e1)
-            q = jnp.where(j == 0, qz(y, e), jnp.where(j == 1, qf(y, e), jnp.where(j == 2, qz(1 - y, e), qf(1 - y, e))))
-            return j, e, q
-
-        def slot_body(slot, cc):
-            @pl.when(slot < 8)
-            def _():
-                j, e, q = slot_q(slot)
-                at_origin = jnp.logical_and(is_end, e == e2)
-                own = jnp.logical_and(at_origin, j < 2)
-                from_y = jnp.logical_or(j == 3, jnp.logical_and(at_origin, j == 2))
-                from_chain = jnp.logical_not(jnp.logical_or(own, from_y))
-                last = jnp.logical_and(is_end, e == e1)
-                fwd = jnp.logical_and(jnp.logical_and(j < 3, jnp.logical_not(last)), jnp.logical_not(own))
-                kind = jnp.where(j == 3, 0, 1)
-                for ch in range(2):
-                    buf = kp.at[0, q, krow(ch), :]
-
-                    @pl.when(from_chain)
-                    def _():
-                        jj = jnp.minimum(j, 2)
-                        rc(buf, buf, kc_s.at[e, jj * 2 + ch], kc_r.at[e, jj * 2 + ch], me).wait_recv()
-
-                    @pl.when(from_y)
-                    def _():
-                        rc(buf, buf, ky_s.at[e, kind, ch], ky_r.at[e, kind, ch], me).wait_recv()
-
-                    @pl.when(fwd)
-                    def _():
-                        kc_copy(e, j, ch, q).start()
-
-                    @pl.when(jnp.logical_and(j == 1, jnp.logical_not(own)))
-                    def _():
-                        ky_copy(e, 0, ch, q).start()
-
-                    @pl.when(jnp.logical_not(own))
-                    def _():
-                        kx_copy(ch, q).start()
-                assemble(0, q)
-
-            @pl.when(slot > 0)
-            def _():
-                _, _, q = slot_q(slot - 1)
-                for ch in range(2):
-                    buf = kp.at[1, q, krow(ch), :]
-                    rc(buf, buf, kx_s.at[q, ch], kx_r.at[q, ch], me).wait_recv()
-                assemble(1, q)
+        def panel_q(j, e):
+            return jnp.where(j == 0, qz(y, e), jnp.where(j == 1, qf(y, e), qz(1 - y, e)))
+
+        def k_take(m, e, fwd):
+            j, ch = m // KCH, m % KCH
+            q = panel_q(j, e)
+            rows = pl.ds(pl.multiple_of(ch * (BLK // KCH), BLK // KCH), BLK // KCH)
+            buf = kp.at[0, q, rows, :]
+            rc(buf, buf, kc_s.at[e, m], kc_r.at[e, m], me).wait_recv()
+            if fwd:
+                rc(buf, buf, kc_s.at[e, m], kc_r.at[e, m], away(e)).start()
+
+            @pl.when(j == 1)
+            def _():
+                rc(buf, buf, ky_s.at[e, 0, ch], ky_r.at[e, 0, ch], ynb).start()
+            rc(buf, kp.at[1, q, rows, :], kx_s.at[q, ch], kx_r.at[q, ch], sib).start()
+
+        def from_sib(q):
+            for ch in range(KCH):
+                buf = kp.at[1, q, krow(ch), :]
+                rc(buf, buf, kx_s.at[q, ch], kx_r.at[q, ch], me).wait_recv()
+            assemble(1, q)
+
+        def from_y(e):
+            q = qf(1 - y, e)
+            for ch in range(KCH):
+                buf = kp.at[0, q, krow(ch), :]
+                rc(buf, buf, ky_s.at[e, 0, ch], ky_r.at[e, 0, ch], me).wait_recv()
+                kx_copy(ch, q).start()
+            assemble(0, q)
+
+        @pl.when(is_end)
+        def _():
+            q = qz(1 - y, e2)
+            for ch in range(KCH):
+                buf = kp.at[0, q, krow(ch), :]
+                rc(buf, buf, ky_s.at[e2, 1, ch], ky_r.at[e2, 1, ch], me).wait_recv()
+                kc_copy(e2, 2, ch, q).start()
+                kx_copy(ch, q).start()
+
+        def k_round(m, cc):
+            near = m < 3 * KCH
+            far = m >= KSKEW
+            nf = jnp.maximum(m - KSKEW, 0)
+            nn = jnp.minimum(m, 3 * KCH - 1)
+
+            @pl.when(jnp.logical_and(near, is_mid))
+            def _():
+                k_take(nn, e2, True)
+
+            @pl.when(jnp.logical_and(far, is_mid))
+            def _():
+                k_take(nf, e1, True)
+
+            @pl.when(jnp.logical_and(far, is_end))
+            def _():
+                k_take(nf, e1, False)
+
+            @pl.when(jnp.logical_and(near, m % KCH == KCH - 1))
+            def _():
+                assemble(0, panel_q(nn // KCH, e2))
+
+            @pl.when(jnp.logical_and(near, jnp.logical_and(m % KCH == KCH - 1, m >= KCH)))
+            def _():
+                from_sib(panel_q(nn // KCH - 1, e2))
+
+            @pl.when(jnp.logical_and(far, nf % KCH == KCH - 1))
+            def _():
+                assemble(0, panel_q(nf // KCH, e1))
+
+            @pl.when(jnp.logical_and(far, jnp.logical_and(nf % KCH == KCH - 1, nf >= KCH)))
+            def _():
+                from_sib(panel_q(nf // KCH - 1, e1))
+
+            @pl.when(m == 2 * KCH + KSKEW)
+            def _():
+                from_y(e2)
             return cc
 
-        lax.fori_loop(0, 9, slot_body, 0)
+        lax.fori_loop(0, 3 * KCH + KSKEW, k_round, 0)
+        from_y(e1)
+
+        def last_sib(k, cc):
+            from_sib(jnp.where(k == 0, panel_q(2, e2), jnp.where(k == 1, qf(1 - y, e2), jnp.where(k == 2, qf(1 - y, e1), panel_q(2, e1)))))
+            return cc
+
+        lax.fori_loop(0, 4, last_sib, 0)
 
         for e in range(2):
             for i in range(NCH):
@@ -356,7 +412,12 @@
             for i in range(NCH):
                 zy_copy(i).wait_send()
 
-        def phi_tile(i, cc):
+        def phi_tile(k, cc):
+            low = z < 2
+            zm = jnp.where(low, z, 3 - z)
+            zo = jnp.where(k < 2, 2, jnp.where(k < 4, 3, jnp.where(k < 6, 1 - zm, zm)))
+            zz = jnp.where(low, zo, 3 - zo)
+            i = ((zz + 4 - 2 * c) % 4) * 2 + k % 2
             h = i // 4
             rows = pl.ds(pl.multiple_of(i * TILE, TILE), TILE)
             krows = pl.ds(pl.multiple_of((i % 4) * TILE, TILE), TILE)
@@ -377,7 +438,6 @@
 
             @pl.when(t == NUM_STEPS - 1)
             def _():
-                zz = (i // 2 + 2 * c) % 4
                 dst = out_ref.at[pl.ds(pl.multiple_of((i % 2) * TILE, TILE), TILE), pl.ds(pl.multiple_of(z * width, BLK), width)]
 
                 @pl.when(zz == z)
@@ -395,7 +455,7 @@
         def _():
             z_copy().start()
 
-        for ch in range(2):
+        for ch in range(KCH):
             for e in range(2):
                 ky_copy(e, 0, ch, qf(y, e)).wait_send()
 
@@ -482,7 +542,7 @@
                 pltpu.VMEM((16, BLK), F32),
                 dma((4,)), dma((4,)), dma((8,)), dma((8,)), dma, dma,
                 dma((2, NCH)), dma((2, NCH)), dma((2, 3 * NCH)), dma((2, 3 * NCH)), dma((NCH,)), dma((NCH,)),
-                dma((2, 6)), dma((2, 6)), dma((2, 2, 2)), dma((2, 2, 2)), dma((8, 2)), dma((8, 2)),
+                dma((2, 3 * KCH)), dma((2, 3 * KCH)), dma((2, 2, KCH)), dma((2, 2, KCH)), dma((8, KCH)), dma((8, KCH)),
                 dma((8,)), dma((4, 2)),
             ],
             compiler_params=pltpu.CompilerParams(collective_id=0, has_side_effects=True, vmem_limit_bytes=63 * 1024 * 1024),

time: 783 us -> 585 us (0.75)
  the two profiles are of different devices: /device:TPU:15 before, /device:TPU:0 now
where the time goes in v2:
time: 585 us; the launch traced here: 584 us
  Pallas kernels  574 us (98%)
  local copies, waits for them, and re-layouts  10 us (2%)
    pallas_call x1, Pallas kernels, local_steps(): pl.pallas_call(body, out_shape=jax.ShapeDtypeStruct((rows_loc, feat_loc),...  574 us

profile of v2, /device:TPU:0, one launch (start us, length us, event | category | flops | bytes accessed | tf_op | source)
XLA Modules:
  0.0 584.2 jit_solution(11479299388235110647)
XLA Ops:
  0.0 0.0 copy-start
  0.0 0.8 dynamic_slice.9
  0.8 0.6 broadcast_in_dim.6.refs_1_
  1.4 0.8 dynamic_slice.10
  2.2 0.6 broadcast_in_dim.7.refs_2_
  2.8 0.0 copy-done
  2.8 0.2 copy.6
  3.0 0.9 fusion
  3.8 574.2 %svgd.1 = f32[512,3072]{1,0:T(8,128)} custom-call(f32[512,3072]{1,0:T(8,128)} %refs_0_.1, f32[1,768]{1,0:T(1,128)} %broadcast_in_dim.6.refs_1_, f32[1,768]{1,0:T(1,128)} %broadcast_in_dim.7.refs_2_, bf16[768,128]{1,0:T(8,128)(2,1)} %get-tuple-element.6.refs_3_, bf16[768,128]{1,0:T(8,128)(2,1)} %get-tuple-element.5.refs_4_), custom_call_target="tpu_custom_call" | custom-call | tf_op jit(solution)/shard_map/svgd/pallas_call | solution.py:523
  578.0 6.2 %copy.8 = f32[512,3072]{1,0:T(8,128)} copy(f32[512,3072]{1,0:T(8,128)} %svgd.1) | data formatting | bytes 12582912
  (1 shorter events, 0.0 us)
Async XLA Ops:
  0.0 2.8 copy-start

commit v3 on v2

--- a/solution.py
+++ b/solution.py
@@ -15,7 +15,8 @@
 CH = BLK // NCH
 KCH = 4
 HR = BLK // 2
-KSKEW = 2
+FSTART = 4
+YFWD = (17, 20, 22, 23)
 SKEW = 3
 TILE = 256
 BF = jnp.bfloat16
@@ -33,8 +34,8 @@
 
 
 def _kernel(n_total, kern_width, step_size,
-            theta_in, prec_ref, mean_ref, u0_ref, u1_ref, out_ref,
-            th, tb, tsib, ab, gp, fr, cr, zr, kp, k2, zown, zsnd, zrcv, sfull,
+            theta_in, prec_in, mean_in, fact_in, out_ref,
+            th, tb, tsib, ab, gp, fr, cr, zr, kp, k2, zall, zrcv, sfull, prec_ref, mean_ref, u0_ref, u1_ref, par_s,
             in_s, in_r, tx_s, tx_r, zx_s, zx_r, fy_s, fy_r, ch_s, ch_r, zy_s, zy_r,
             kc_s, kc_r, ky_s, ky_r, kx_s, kx_r, out_s, out_r):
     z = lax.axis_index("part")
@@ -73,6 +74,13 @@
     pl.semaphore_signal(bar, inc=1, device_id=sib, device_id_type=MESH)
     pl.semaphore_wait(bar, 5)
 
+    mine = pl.ds(pl.multiple_of(z * width, BLK), width)
+    rank = fact_in.shape[0]
+    pars = (pltpu.make_async_copy(prec_in.at[:, mine], prec_ref, par_s.at[0]),
+            pltpu.make_async_copy(mean_in.at[:, mine], mean_ref, par_s.at[1]),
+            pltpu.make_async_copy(fact_in.at[:, mine], u0_ref.at[pl.ds(0, rank), :], par_s.at[2]),
+            pltpu.make_async_copy(fact_in.at[:, mine], u1_ref.at[pl.ds(HR, rank), :], par_s.at[3]))
+
     def grp(zz):
         return pl.multiple_of(((zz + 4 - 2 * c) % 4) * group, group)
 
@@ -91,13 +99,23 @@
             def _(zz=zz):
                 in_copy(zz).start()
 
+    for p in pars:
+        p.start()
+    u0_ref[HR:BLK, :] = jnp.zeros((HR, width), BF)
+    u1_ref[0:HR, :] = jnp.zeros((HR, width), BF)
+    if rank < HR:
+        u0_ref[rank:HR, :] = jnp.zeros((HR - rank, width), BF)
+        u1_ref[HR + rank:BLK, :] = jnp.zeros((HR - rank, width), BF)
+    for p in pars:
+        p.wait()
+
     def t_copy(par, i):
         src = tb.at[par, pl.ds(pl.multiple_of(i * TILE, TILE), TILE), :]
         dst = tsib.at[pl.ds(pl.multiple_of(((i + 4) % 8) * TILE, TILE), TILE), :]
         return rc(src, dst, tx_s.at[i], tx_r.at[(i + 4) % 8], sib)
 
     def z_copy():
-        return rc(zsnd, zrcv, zx_s, zx_r, sib)
+        return rc(zall.at[pl.ds(8, 9)], zrcv, zx_s, zx_r, sib)
 
     eye = (lax.broadcasted_iota(jnp.int32, (BLK, BLK), 0) == lax.broadcasted_iota(jnp.int32, (BLK, BLK), 1))
 
@@ -105,23 +123,16 @@
         rows = pl.ds(pl.multiple_of(i * TILE, TILE), TILE)
         tt = th[rows, :].astype(BF)
         tb[par, rows, :] = tt
-        t_copy(par, i).start()
+        z_tile = _dot_nt((th[rows, :] - mean_ref[...]).astype(BF), u0_ref[...])
+        low_lanes = lax.broadcasted_iota(jnp.int32, (HR, BLK), 1) < HR
         for s in range(TILE // BLK):
             b = i * (TILE // BLK) + s
             t_blk = tt[s * BLK:(s + 1) * BLK].astype(F32)
             s_col = jnp.sum(t_blk * t_blk, axis=1, keepdims=True)
             s_row = jnp.sum(jnp.where(eye, jnp.broadcast_to(s_col, (BLK, BLK)), 0.0), axis=0, keepdims=True)
-            zsnd[8, pl.ds(b, 1), :] = s_row
-            x_blk = (th[pl.ds(pl.multiple_of(b * BLK, BLK), BLK), :] - mean_ref[...]).astype(BF)
-            zq = _dot(x_blk[:BLK // 2], u0_ref[...]) + _dot(x_blk[BLK // 2:], u1_ref[...])
-
-            @pl.when(b < 8)
-            def _():
-                zown[b] = zq
-
-            @pl.when(b >= 8)
-            def _():
-                zsnd[b - 8] = zq
+            zall[16, pl.ds(b, 1), :] = s_row
+            z_blk = z_tile[s * BLK:(s + 1) * BLK]
+            zall[b] = jnp.where(low_lanes, z_blk[:HR], pltpu.roll(z_blk[HR:], HR, 1))
 
     def first_rows(k, carry):
         zz = (z + k) % 4
@@ -134,7 +145,9 @@
         def _():
             rc(th.at[pl.ds(grp(zz), group), :], th.at[pl.ds(grp(zz), group), :], in_s.at[zz], in_r.at[zz], me).wait_recv()
         for s in range(group // TILE):
-            finish_rows(((zz + 4 - 2 * c) % 4) * (group // TILE) + s, 0)
+            i = ((zz + 4 - 2 * c) % 4) * (group // TILE) + s
+            finish_rows(i, 0)
+            t_copy(0, i).start()
         return carry
 
     lax.fori_loop(0, 4, first_rows, 0)
@@ -184,15 +197,15 @@
 
         lax.fori_loop(0, 8, t_wait, 0)
         z_copy().wait()
-        sfull[0:8, :] = zsnd[8, 0:8, :] + zrcv[8, 8:16, :]
-        sfull[8:16, :] = zsnd[8, 8:16, :] + zrcv[8, 0:8, :]
+        sfull[0:8, :] = zall[16, 0:8, :] + zrcv[8, 8:16, :]
+        sfull[8:16, :] = zall[16, 8:16, :] + zrcv[8, 0:8, :]
 
         def panel(q):
             rows = pl.ds(pl.multiple_of(q * BLK, BLK), BLK)
             win = pl.ds(pl.multiple_of(q * BLK, BLK), GW)
             gp[q, :, 0:GW] = _dot_nt(tb[par, rows, :], tb[par, win, :]) + _dot_nt(tsib[rows, :], tsib[win, :])
             gp[q, 0:16, GW:PW] = sfull[...]
-            gp[q, 16:80, GW:PW] = zown[q] + zrcv[q]
+            gp[q, 16:80, GW:PW] = zall[q] + zrcv[q]
             gp[q, 80:BLK, GW:PW] = jnp.zeros((BLK - 80, BLK), F32)
 
         def mk_panels(m, cc):
@@ -200,7 +213,7 @@
             e = jnp.where(k % 2 == 0, e1, e2)
             panel(jnp.where(k < 2, qf(1 - y, e), qz(1 - y, e)))
 
-            @pl.when(k < 2)
+            @pl.when(jnp.logical_and(k < 2, jnp.logical_or(is_mid, k == 0)))
             def _():
                 for i in range(NCH):
                     fy_copy(e, i).start()
@@ -223,20 +236,27 @@
                     chain_copy(NCH + i, e1).start()
             return cc
 
-        def kern_panel(q):
-            s_col = jnp.sum(jnp.where(eye, jnp.broadcast_to(sfull[pl.ds(q, 1), :], (BLK, BLK)), 0.0), axis=1, keepdims=True)
+        KR = BLK // KCH
+
+        def kern_chunk(q, ch):
+            rows = slice(ch * KR, (ch + 1) * KR)
+            diag = lax.broadcasted_iota(jnp.int32, (KR, BLK), 0) + ch * KR == lax.broadcasted_iota(jnp.int32, (KR, BLK), 1)
+            s_col = jnp.sum(jnp.where(diag, jnp.broadcast_to(sfull[pl.ds(q, 1), :], (KR, BLK)), 0.0), axis=1, keepdims=True)
             for k in range(SPAN):
                 cols = slice(k * BLK, (k + 1) * BLK)
-                dist = jnp.maximum(s_col + sfull[pl.ds(q + k, 1), :] - 2.0 * gp[q, :, cols], 0.0)
-                kp[0, q, :, cols] = jnp.exp(dist * (-1.0 / kern_width)).astype(BF)
-            kp[0, q, 0:HR, GW:PW] = jnp.zeros((HR, BLK), BF)
-            kp[0, q, HR:BLK, GW:PW] = gp[q, 16:80, GW:PW].astype(BF)
-
-        def send_own(j, q):
-            for ch in range(KCH):
-                kc_copy(e2, j, ch, q).start()
-                ky_copy(e2, 1 - j, ch, q).start()
-                kx_copy(ch, q).start()
+                dist = jnp.maximum(s_col + sfull[pl.ds(q + k, 1), :] - 2.0 * gp[q, rows, cols], 0.0)
+                kp[0, q, rows, cols] = jnp.exp(dist * (-1.0 / kern_width)).astype(BF)
+            if ch < KCH // 2:
+                kp[0, q, rows, GW:PW] = jnp.zeros((KR, BLK), BF)
+            else:
+                zr0 = 16 + (ch - KCH // 2) * KR
+                kp[0, q, rows, GW:PW] = gp[q, zr0:zr0 + KR, GW:PW].astype(BF)
+
+        def send_own(j, q, ch):
+            kern_chunk(q, ch)
+            kc_copy(e2, j, ch, q).start()
+            ky_copy(e2, 1 if j == 0 else 0, ch, q).start()
+            kx_copy(ch, q).start()
 
         def take(n, e, with_chain, with_y):
             i = n % NCH
@@ -251,34 +271,63 @@
                 val = val + cr[e, n]
             gp[q, rows, :] = val
 
+        def panel_q(j, e):
+            return jnp.where(j == 0, qz(y, e), jnp.where(j == 1, qf(y, e), qz(1 - y, e)))
+
+        def k_take(m, e, fwd):
+            j, ch = m // KCH, m % KCH
+            q = panel_q(j, e)
+            rows = pl.ds(pl.multiple_of(ch * (BLK // KCH), BLK // KCH), BLK // KCH)
+            buf = kp.at[0, q, rows, :]
+            rc(buf, buf, kc_s.at[e, m], kc_r.at[e, m], me).wait_recv()
+            if fwd:
+                rc(buf, buf, kc_s.at[e, m], kc_r.at[e, m], away(e)).start()
+
+            @pl.when(j == 1)
+            def _():
+                rc(buf, buf, ky_s.at[e, 0, ch], ky_r.at[e, 0, ch], ynb).start()
+            rc(buf, kp.at[1, q, rows, :], kx_s.at[q, ch], kx_r.at[q, ch], sib).start()
+
         def mid_round(m):
             for n, e in ((m, e1), (m - SKEW, e2)):
                 if 0 <= n < 3 * NCH:
                     take(n, e, True, n >= 2 * NCH)
                     chain_copy(n, e).start()
+                elif n >= 3 * NCH:
+                    k_take(jnp.int32(n - 3 * NCH), e2, True)
 
         def end_round(n):
-            i = n % NCH
-            rows = crow(i)
-            if NCH <= n < 2 * NCH:
-                take(n + NCH, e1, False, True)
-                chain_copy(n + NCH, e1).start()
+            if FSTART <= n < FSTART + NCH // 2:
+                for k in range(2):
+                    nn = 2 * NCH + 2 * (n - FSTART) + k
+                    take(nn, e1, False, True)
+                    chain_copy(nn, e1).start()
             take(n, e2, True, n >= 2 * NCH)
             if n < NCH:
-                zy_copy(i).start()
-            elif n < 2 * NCH:
+                zy_copy(n).start()
+            if NCH <= n < 2 * NCH:
+                i = n - NCH
+                rows = crow(i)
                 rc(zr.at[rows, :], zr.at[rows, :], zy_s.at[i], zy_r.at[i], me).wait_recv()
                 q = qz(y, e2)
                 gp[q, rows, :] = gp[q, rows, :] + zr[rows, :]
-            if n == 2 * NCH - 1:
-                q = qz(y, e2)
-                sfull[...] = gp[q, 0:16, GW:PW]
-                kern_panel(q)
-                send_own(0, q)
-            if n == 3 * NCH - 1:
-                q = qf(y, e2)
-                kern_panel(q)
-                send_own(1, q)
+                if n == NCH:
+                    sfull[...] = gp[q, 0:16, GW:PW]
+            if NCH - 1 <= n < 2 * NCH - 1:
+                fy_copy(e2, n - NCH + 1).start()
+            per = NCH // KCH
+            if n >= NCH and n % per == per - 1:
+                if n < 2 * NCH:
+                    send_own(0, qz(y, e2), (n - NCH) // per)
+                else:
+                    send_own(1, qf(y, e2), (n - 2 * NCH) // per)
+            if n in YFWD:
+                ch = YFWD.index(n)
+                q = qz(1 - y, e2)
+                buf = kp.at[0, q, krow(ch), :]
+                rc(buf, buf, ky_s.at[e2, 1, ch], ky_r.at[e2, 1, ch], me).wait_recv()
+                kc_copy(e2, 2, ch, q).start()
+                kx_copy(ch, q).start()
 
         @pl.when(is_mid)
         def _():
@@ -305,26 +354,9 @@
             zb = kp[h, q, HR:BLK, GW:PW]
             for s, u_ref in ((0, u0_ref), (1, u1_ref)):
                 rows = pl.ds(pl.multiple_of((h * 8 + q) * BLK + s * HR, HR), HR)
-                low = _dot_nt(zb, u_ref[...])
+                low = _dot(zb, u_ref[...])
                 x_dev = th[rows, :] - mean_ref[...]
                 ab[rows, :] = (-(x_dev * prec_ref[...] + low)).astype(BF)
-
-        def panel_q(j, e):
-            return jnp.where(j == 0, qz(y, e), jnp.where(j == 1, qf(y, e), qz(1 - y, e)))
-
-        def k_take(m, e, fwd):
-            j, ch = m // KCH, m % KCH
-            q = panel_q(j, e)
-            rows = pl.ds(pl.multiple_of(ch * (BLK // KCH), BLK // KCH), BLK // KCH)
-            buf = kp.at[0, q, rows, :]
-            rc(buf, buf, kc_s.at[e, m], kc_r.at[e, m], me).wait_recv()
-            if fwd:
-                rc(buf, buf, kc_s.at[e, m], kc_r.at[e, m], away(e)).start()
-
-            @pl.when(j == 1)
-            def _():
-                rc(buf, buf, ky_s.at[e, 0, ch], ky_r.at[e, 0, ch], ynb).start()
-            rc(buf, kp.at[1, q, rows, :], kx_s.at[q, ch], kx_r.at[q, ch], sib).start()
 
         def from_sib(q):
             for ch in range(KCH):
@@ -340,59 +372,45 @@
                 kx_copy(ch, q).start()
             assemble(0, q)
 
-        @pl.when(is_end)
-        def _():
-            q = qz(1 - y, e2)
-            for ch in range(KCH):
-                buf = kp.at[0, q, krow(ch), :]
-                rc(buf, buf, ky_s.at[e2, 1, ch], ky_r.at[e2, 1, ch], me).wait_recv()
-                kc_copy(e2, 2, ch, q).start()
-                kx_copy(ch, q).start()
-
         def k_round(m, cc):
-            near = m < 3 * KCH
-            far = m >= KSKEW
-            nf = jnp.maximum(m - KSKEW, 0)
-            nn = jnp.minimum(m, 3 * KCH - 1)
+            near = m + SKEW < 3 * KCH
+            nn = jnp.minimum(m + SKEW, 3 * KCH - 1)
 
             @pl.when(jnp.logical_and(near, is_mid))
             def _():
                 k_take(nn, e2, True)
 
-            @pl.when(jnp.logical_and(far, is_mid))
-            def _():
-                k_take(nf, e1, True)
-
-            @pl.when(jnp.logical_and(far, is_end))
-            def _():
-                k_take(nf, e1, False)
-
-            @pl.when(jnp.logical_and(near, m % KCH == KCH - 1))
+            @pl.when(is_mid)
+            def _():
+                k_take(m, e1, True)
+
+            @pl.when(is_end)
+            def _():
+                k_take(m, e1, False)
+
+            @pl.when(jnp.logical_and(near, nn % KCH == KCH - 1))
             def _():
                 assemble(0, panel_q(nn // KCH, e2))
 
-            @pl.when(jnp.logical_and(near, jnp.logical_and(m % KCH == KCH - 1, m >= KCH)))
+            @pl.when(jnp.logical_and(near, jnp.logical_and(nn % KCH == KCH - 1, nn >= KCH)))
             def _():
                 from_sib(panel_q(nn // KCH - 1, e2))
 
-            @pl.when(jnp.logical_and(far, nf % KCH == KCH - 1))
-            def _():
-                assemble(0, panel_q(nf // KCH, e1))
-
-            @pl.when(jnp.logical_and(far, jnp.logical_and(nf % KCH == KCH - 1, nf >= KCH)))
-            def _():
-                from_sib(panel_q(nf // KCH - 1, e1))
-
-            @pl.when(m == 2 * KCH + KSKEW)
-            def _():
-                from_y(e2)
+            @pl.when(m % KCH == KCH - 1)
+            def _():
+                assemble(0, panel_q(m // KCH, e1))
+
+            @pl.when(jnp.logical_and(m % KCH == KCH - 1, m >= KCH))
+            def _():
+                from_sib(panel_q(m // KCH - 1, e1))
             return cc
 
-        lax.fori_loop(0, 3 * KCH + KSKEW, k_round, 0)
+        lax.fori_loop(0, 3 * KCH, k_round, 0)
+        from_y(e2)
         from_y(e1)
 
         def last_sib(k, cc):
-            from_sib(jnp.where(k == 0, panel_q(2, e2), jnp.where(k == 1, qf(1 - y, e2), jnp.where(k == 2, qf(1 - y, e1), panel_q(2, e1)))))
+            from_sib(jnp.where(k == 0, qf(1 - y, e2), jnp.where(k == 1, qf(1 - y, e1), jnp.where(k == 2, panel_q(2, e2), panel_q(2, e1)))))
             return cc
 
         lax.fori_loop(0, 4, last_sib, 0)
@@ -412,12 +430,17 @@
             for i in range(NCH):
                 zy_copy(i).wait_send()
 
-        def phi_tile(k, cc):
+        def tile_of(k):
             low = z < 2
             zm = jnp.where(low, z, 3 - z)
             zo = jnp.where(k < 2, 2, jnp.where(k < 4, 3, jnp.where(k < 6, 1 - zm, zm)))
             zz = jnp.where(low, zo, 3 - zo)
-            i = ((zz + 4 - 2 * c) % 4) * 2 + k % 2
+            return zz, ((zz + 4 - 2 * c) % 4) * 2 + k % 2
+
+        def phi_tile(k, cc):
+            zz, i = tile_of(k)
+            _, done = tile_of(jnp.maximum(k - 1, 0))
+            finish_rows(done, 1 - par)
             h = i // 4
             rows = pl.ds(pl.multiple_of(i * TILE, TILE), TILE)
             krows = pl.ds(pl.multiple_of((i % 4) * TILE, TILE), TILE)
@@ -432,9 +455,9 @@
             upd = (drive + (2.0 / kern_width) * (mass * t_own - pull)) * (1.0 / n_total)
             th[rows, :] = th[rows, :] + step_size * upd
 
-            @pl.when(t < NUM_STEPS - 1)
-            def _():
-                finish_rows(i, 1 - par)
+            @pl.when(jnp.logical_and(t < NUM_STEPS - 1, k > 0))
+            def _():
+                t_copy(1 - par, done).start()
 
             @pl.when(t == NUM_STEPS - 1)
             def _():
@@ -453,6 +476,9 @@
 
         @pl.when(t < NUM_STEPS - 1)
         def _():
+            _, done = tile_of(7)
+            finish_rows(done, 1 - par)
+            t_copy(1 - par, done).start()
             z_copy().start()
 
         for ch in range(KCH):
@@ -509,21 +535,13 @@
         width = feat_loc // part_size
         kern_width = 2.0 * feat_total / math.log(n_total)
         step_size = 0.15 * n_total * feat_total / math.log(n_total)
-        start = lax.axis_index("part") * width
-        prec = lax.dynamic_slice_in_dim(prec_loc, start, width)[None, :]
-        mean = lax.dynamic_slice_in_dim(mean_loc, start, width)[None, :]
-        factor = lax.dynamic_slice_in_dim(factor_loc, start, width)
-        rank = factor.shape[1]
-        u0 = jnp.pad(factor, ((0, 0), (0, BLK - rank)))
-        u1 = jnp.pad(factor, ((0, 0), (BLK - rank, 0)))
-        vmem = pl.BlockSpec(memory_space=pltpu.VMEM)
         anym = pl.BlockSpec(memory_space=pl.ANY)
         dma = pltpu.SemaphoreType.DMA
         body = lambda *refs: _kernel(n_total, kern_width, step_size, *refs)
         return pl.pallas_call(
             body,
             out_shape=jax.ShapeDtypeStruct((rows_loc, feat_loc), F32),
-            in_specs=[anym, vmem, vmem, vmem, vmem],
+            in_specs=[anym, anym, anym, anym],
             out_specs=anym,
             scratch_shapes=[
                 pltpu.VMEM((n_total, width), F32),
@@ -536,10 +554,12 @@
                 pltpu.VMEM((BLK, PW), F32),
                 pltpu.VMEM((2, 8, BLK, PW), BF),
                 pltpu.VMEM((2, n_total // 2, n_total), BF),
-                pltpu.VMEM((8, BLK // 2, BLK), F32),
-                pltpu.VMEM((9, BLK // 2, BLK), F32),
-                pltpu.VMEM((9, BLK // 2, BLK), F32),
+                pltpu.VMEM((17, HR, BLK), F32),
+                pltpu.VMEM((9, HR, BLK), F32),
                 pltpu.VMEM((16, BLK), F32),
+                pltpu.VMEM((1, width), F32), pltpu.VMEM((1, width), F32),
+                pltpu.VMEM((BLK, width), BF), pltpu.VMEM((BLK, width), BF),
+                dma((4,)),
                 dma((4,)), dma((4,)), dma((8,)), dma((8,)), dma, dma,
                 dma((2, NCH)), dma((2, NCH)), dma((2, 3 * NCH)), dma((2, 3 * NCH)), dma((NCH,)), dma((NCH,)),
                 dma((2, 3 * KCH)), dma((2, 3 * KCH)), dma((2, 2, KCH)), dma((2, 2, KCH)), dma((8, KCH)), dma((8, KCH)),
@@ -547,7 +567,7 @@
             ],
             compiler_params=pltpu.CompilerParams(collective_id=0, has_side_effects=True, vmem_limit_bytes=63 * 1024 * 1024),
             name="svgd",
-        )(local_theta, prec, mean, u0, u1)
+        )(local_theta, prec_loc[None, :], mean_loc[None, :], factor_loc.T)
 
     row_spec = P(("ens", "part"), "feat")
     vec_spec = P(("ens", "feat"))

time: 585 us -> 571 us (0.976)
  Pallas kernels: 574 us -> 565 us
    pallas_call x1, Pallas kernels: 574 us -> 565 us  [local_steps(): pl.pallas_call(body, out_shape=jax.ShapeDtypeStruct((rows_loc, feat_loc),...]
where the time goes in v3:
time: 571 us
  Pallas kernels  565 us (99%)
  local copies, waits for them, and re-layouts  6.23 us (1%)
    pallas_call x1, Pallas kernels, local_steps(): pl.pallas_call(body, out_shape=jax.ShapeDtypeStruct((rows_loc, feat_loc),...  565 us

profile of v3, /device:TPU:0, one launch (start us, length us, event | category | flops | bytes accessed | tf_op | source)
XLA Modules:
  0.0 570.8 jit_solution(4810519768420879378)
XLA Ops:
  0.0 564.6 %svgd.1 = f32[512,3072]{1,0:T(8,128)} custom-call(f32[512,3072]{1,0:T(8,128)} %refs_0_.1, f32[1,3072]{1,0:T(1,128)} %bitcast.4, f32[1,3072]{1,0:T(1,128)} %bitcast.5, bf16[64,3072]{1,0:T(8,128)(2,1)} %bitcast.3), custom_call_target="tpu_custom_call" | custom-call | tf_op jit(solution)/shard_map/svgd/pallas_call | solution.py:541
  564.6 6.2 %copy.6 = f32[512,3072]{1,0:T(8,128)} copy(f32[512,3072]{1,0:T(8,128)} %svgd.1) | data formatting | bytes 12582912

commit v4 on v3

--- a/solution.py
+++ b/solution.py
@@ -8,7 +8,7 @@
 
 NUM_STEPS = 3
 BLK = 128
-SPAN = 9
+SPAN = 8
 PW = (SPAN + 1) * BLK
 GW = SPAN * BLK
 NCH = 8
@@ -35,7 +35,7 @@
 
 def _kernel(n_total, kern_width, step_size,
             theta_in, prec_in, mean_in, fact_in, out_ref,
-            th, tb, tsib, ab, gp, fr, cr, zr, kp, k2, zall, zrcv, sfull, prec_ref, mean_ref, u0_ref, u1_ref, par_s,
+            th, tb, tsib, ab, gp, fr, cr, zr, kp, k2, zall, zrcv, sfull, sown, sbuf, prec_ref, mean_ref, u0_ref, u1_ref, par_s, sx_s, sx_r,
             in_s, in_r, tx_s, tx_r, zx_s, zx_r, fy_s, fy_r, ch_s, ch_r, zy_s, zy_r,
             kc_s, kc_r, ky_s, ky_r, kx_s, kx_r, out_s, out_r):
     z = lax.axis_index("part")
@@ -70,9 +70,10 @@
     bar = pltpu.get_barrier_semaphore()
     for k in range(1, 4):
         pl.semaphore_signal(bar, inc=1, device_id=dev((z + k) % 4, y, c), device_id_type=MESH)
-    pl.semaphore_signal(bar, inc=1, device_id=ynb, device_id_type=MESH)
+    for k in range(4):
+        pl.semaphore_signal(bar, inc=1, device_id=dev((z + k) % 4, 1 - y, c), device_id_type=MESH)
     pl.semaphore_signal(bar, inc=1, device_id=sib, device_id_type=MESH)
-    pl.semaphore_wait(bar, 5)
+    pl.semaphore_wait(bar, 8)
 
     mine = pl.ds(pl.multiple_of(z * width, BLK), width)
     rank = fact_in.shape[0]
@@ -167,6 +168,9 @@
     def fy_copy(e, i):
         return rc(gp.at[qf(1 - y, e), crow(i), :], fr.at[e, crow(i), :], fy_s.at[e, i], fy_r.at[e, i], ynb)
 
+    def s_copy(yy, e, k):
+        return rc(sown, sbuf.at[2 * z + y], sx_s.at[k], sx_r.at[2 * z + y], dev(3 * e, yy, c))
+
     def chain_q(n, e):
         return (qz(1 - y, e), qz(y, e), qf(y, e))[n // NCH]
 
@@ -197,16 +201,24 @@
 
         lax.fori_loop(0, 8, t_wait, 0)
         z_copy().wait()
-        sfull[0:8, :] = zall[16, 0:8, :] + zrcv[8, 8:16, :]
-        sfull[8:16, :] = zall[16, 8:16, :] + zrcv[8, 0:8, :]
+        sown[0:8, :] = zall[16, 0:8, :] + zrcv[8, 8:16, :]
+        sown[8:16, :] = zall[16, 8:16, :] + zrcv[8, 0:8, :]
+        for e in range(2):
+            s_copy(1 - y, e, 2 + e).start()
+
+            @pl.when(z != 3 * e)
+            def _(e=e):
+                s_copy(y, e, e).start()
 
         def panel(q):
             rows = pl.ds(pl.multiple_of(q * BLK, BLK), BLK)
-            win = pl.ds(pl.multiple_of(q * BLK, BLK), GW)
-            gp[q, :, 0:GW] = _dot_nt(tb[par, rows, :], tb[par, win, :]) + _dot_nt(tsib[rows, :], tsib[win, :])
-            gp[q, 0:16, GW:PW] = sfull[...]
-            gp[q, 16:80, GW:PW] = zall[q] + zrcv[q]
-            gp[q, 80:BLK, GW:PW] = jnp.zeros((BLK - 80, BLK), F32)
+            win = pl.ds(pl.multiple_of(q * BLK, BLK), PW)
+            gram = _dot_nt(tb[par, rows, :], tb[par, win, :]) + _dot_nt(tsib[rows, :], tsib[win, :])
+            gp[q, :, 0:GW] = gram[:, 0:GW]
+            last = gram[:, GW:PW]
+            right = jnp.logical_and(c == 1, lax.broadcasted_iota(jnp.int32, (HR, BLK), 1) < HR)
+            gp[q, 0:HR, GW:PW] = jnp.where(right, pltpu.roll(last[HR:], HR, 1), last[:HR])
+            gp[q, HR:BLK, GW:PW] = zall[q] + zrcv[q]
 
         def mk_panels(m, cc):
             k = jnp.where(is_end, jnp.where(m == 0, 2, jnp.where(m < 3, m - 1, 3)), m)
@@ -238,19 +250,26 @@
 
         KR = BLK // KCH
 
+        def s_column(q, first):
+            diag = lax.broadcasted_iota(jnp.int32, (KR, BLK), 0) + first == lax.broadcasted_iota(jnp.int32, (KR, BLK), 1)
+            return jnp.sum(jnp.where(diag, jnp.broadcast_to(sfull[pl.ds(q, 1), :], (KR, BLK)), 0.0), axis=1, keepdims=True)
+
+        def kern(s_col, s_row, gram):
+            return jnp.exp(jnp.maximum(s_col + s_row - 2.0 * gram, 0.0) * (-1.0 / kern_width)).astype(BF)
+
         def kern_chunk(q, ch):
             rows = slice(ch * KR, (ch + 1) * KR)
-            diag = lax.broadcasted_iota(jnp.int32, (KR, BLK), 0) + ch * KR == lax.broadcasted_iota(jnp.int32, (KR, BLK), 1)
-            s_col = jnp.sum(jnp.where(diag, jnp.broadcast_to(sfull[pl.ds(q, 1), :], (KR, BLK)), 0.0), axis=1, keepdims=True)
+            s_col = s_column(q, ch * KR)
             for k in range(SPAN):
                 cols = slice(k * BLK, (k + 1) * BLK)
-                dist = jnp.maximum(s_col + sfull[pl.ds(q + k, 1), :] - 2.0 * gp[q, rows, cols], 0.0)
-                kp[0, q, rows, cols] = jnp.exp(dist * (-1.0 / kern_width)).astype(BF)
+                kp[0, q, rows, cols] = kern(s_col, sfull[pl.ds(q + k, 1), :], gp[q, rows, cols])
             if ch < KCH // 2:
-                kp[0, q, rows, GW:PW] = jnp.zeros((KR, BLK), BF)
+                right = jnp.logical_and(c == 1, lax.broadcasted_iota(jnp.int32, (KR, BLK), 1) < HR)
+                s_row = jnp.broadcast_to(sfull[pl.ds(q + SPAN, 1), :], (KR, BLK))
+                kp[0, q, rows, GW:PW] = kern(jnp.where(right, s_column(q, HR + ch * KR), s_col),
+                                             jnp.where(right, pltpu.roll(s_row, HR, 1), s_row), gp[q, rows, GW:PW])
             else:
-                zr0 = 16 + (ch - KCH // 2) * KR
-                kp[0, q, rows, GW:PW] = gp[q, zr0:zr0 + KR, GW:PW].astype(BF)
+                kp[0, q, rows, GW:PW] = gp[q, rows, GW:PW].astype(BF)
 
         def send_own(j, q, ch):
             kern_chunk(q, ch)
@@ -312,7 +331,12 @@
                 q = qz(y, e2)
                 gp[q, rows, :] = gp[q, rows, :] + zr[rows, :]
                 if n == NCH:
-                    sfull[...] = gp[q, 0:16, GW:PW]
+                    sfull[...] = sown[...]
+                    for k in range(8):
+                        @pl.when(2 * z + y != k)
+                        def _(k=k):
+                            rc(sbuf.at[k], sbuf.at[k], sx_s.at[0], sx_r.at[k], me).wait_recv()
+                            sfull[...] = sfull[...] + sbuf[k]
             if NCH - 1 <= n < 2 * NCH - 1:
                 fy_copy(e2, n - NCH + 1).start()
             per = NCH // KCH
@@ -347,7 +371,7 @@
             for k in range(SPAN):
                 blk = kp[h, q, :, k * BLK:(k + 1) * BLK]
                 k2[h, lo, pl.ds(pl.multiple_of((q + k) * BLK, BLK), BLK)] = blk
-                if 1 <= k <= 7:
+                if k >= 1:
                     flip = (q + k) // 8
                     k2[(h + flip) % 2, pl.ds(pl.multiple_of((q + k - 8 * flip) * BLK, BLK), BLK),
                        pl.ds(pl.multiple_of((q + 8 * flip) * BLK, BLK), BLK)] = blk.T
@@ -358,11 +382,22 @@
                 x_dev = th[rows, :] - mean_ref[...]
                 ab[rows, :] = (-(x_dev * prec_ref[...] + low)).astype(BF)
 
+        def pair_block(q):
+            upper = kp[c, q, 0:HR, GW:PW].astype(F32)
+            right = kp[1 - c, q, 0:HR, GW:PW].astype(F32)
+            lower = jnp.concatenate([right, pltpu.roll(right, HR, 1)], axis=0).T[HR:BLK]
+            blk = jnp.concatenate([upper, lower], axis=0)
+            rows = pl.ds(pl.multiple_of(q * BLK, BLK), BLK)
+            cols = pl.ds(pl.multiple_of((q + SPAN) * BLK, BLK), BLK)
+            k2[c, rows, cols] = blk.astype(BF)
+            k2[1 - c, rows, cols] = blk.T.astype(BF)
+
         def from_sib(q):
             for ch in range(KCH):
                 buf = kp.at[1, q, krow(ch), :]
                 rc(buf, buf, kx_s.at[q, ch], kx_r.at[q, ch], me).wait_recv()
             assemble(1, q)
+            pair_block(q)
 
         def from_y(e):
             q = qf(1 - y, e)
@@ -416,6 +451,11 @@
         lax.fori_loop(0, 4, last_sib, 0)
 
         for e in range(2):
+            s_copy(1 - y, e, 2 + e).wait_send()
+
+            @pl.when(z != 3 * e)
+            def _(e=e):
+                s_copy(y, e, e).wait_send()
             for i in range(NCH):
                 fy_copy(e, i).wait_send()
         for n in range(3 * NCH):
@@ -556,10 +596,10 @@
                 pltpu.VMEM((2, n_total // 2, n_total), BF),
                 pltpu.VMEM((17, HR, BLK), F32),
                 pltpu.VMEM((9, HR, BLK), F32),
-                pltpu.VMEM((16, BLK), F32),
+                pltpu.VMEM((16, BLK), F32), pltpu.VMEM((16, BLK), F32), pltpu.VMEM((8, 16, BLK), F32),
                 pltpu.VMEM((1, width), F32), pltpu.VMEM((1, width), F32),
                 pltpu.VMEM((BLK, width), BF), pltpu.VMEM((BLK, width), BF),
-                dma((4,)),
+                dma((4,)), dma((4,)), dma((8,)),
                 dma((4,)), dma((4,)), dma((8,)), dma((8,)), dma, dma,
                 dma((2, NCH)), dma((2, NCH)), dma((2, 3 * NCH)), dma((2, 3 * NCH)), dma((NCH,)), dma((NCH,)),
                 dma((2, 3 * KCH)), dma((2, 3 * KCH)), dma((2, 2, KCH)), dma((2, 2, KCH)), dma((8, KCH)), dma((8, KCH)),

time: 571 us -> 553 us (0.968)
  Pallas kernels: 565 us -> 547 us
    pallas_call x1, Pallas kernels: 565 us -> 547 us  [local_steps(): pl.pallas_call(body, out_shape=jax.ShapeDtypeStruct((rows_loc, feat_loc),...]
where the time goes in v4:
time: 553 us
  Pallas kernels  547 us (99%)
  local copies, waits for them, and re-layouts  6.23 us (1%)
    pallas_call x1, Pallas kernels, local_steps(): pl.pallas_call(body, out_shape=jax.ShapeDtypeStruct((rows_loc, feat_loc),...  547 us

profile of v4, /device:TPU:0, one launch (start us, length us, event | category | flops | bytes accessed | tf_op | source)
XLA Modules:
  0.0 552.8 jit_solution(18311956567504588970)
XLA Ops:
  0.0 546.6 %svgd.1 = f32[512,3072]{1,0:T(8,128)} custom-call(f32[512,3072]{1,0:T(8,128)} %refs_0_.1, f32[1,3072]{1,0:T(1,128)} %bitcast.4, f32[1,3072]{1,0:T(1,128)} %bitcast.5, bf16[64,3072]{1,0:T(8,128)(2,1)} %bitcast.3), custom_call_target="tpu_custom_call" | custom-call | tf_op jit(solution)/shard_map/svgd/pallas_call | solution.py:581
  546.6 6.2 %copy.6 = f32[512,3072]{1,0:T(8,128)} copy(f32[512,3072]{1,0:T(8,128)} %svgd.1) | data formatting | bytes 12582912

commit v5 on v4

--- a/solution.py
+++ b/solution.py
@@ -195,10 +195,17 @@
     def step(t, carry):
         par = t % 2
 
+        def own_part(q):
+            rows = pl.ds(pl.multiple_of(q * BLK, BLK), BLK)
+            win = pl.ds(pl.multiple_of(q * BLK, BLK), PW)
+            return _dot_nt(tb[par, rows, :], tb[par, win, :])
+
         def t_wait(i, cc):
             t_copy(par, i).wait()
             return cc
 
+        first_q = qz(1 - y, e1)
+        gp[first_q] = own_part(first_q)
         lax.fori_loop(0, 8, t_wait, 0)
         z_copy().wait()
         sown[0:8, :] = zall[16, 0:8, :] + zrcv[8, 8:16, :]
@@ -210,33 +217,34 @@
             def _(e=e):
                 s_copy(y, e, e).start()
 
-        def panel(q):
+        def panel(q, gram=None):
             rows = pl.ds(pl.multiple_of(q * BLK, BLK), BLK)
             win = pl.ds(pl.multiple_of(q * BLK, BLK), PW)
-            gram = _dot_nt(tb[par, rows, :], tb[par, win, :]) + _dot_nt(tsib[rows, :], tsib[win, :])
+            gram = (own_part(q) if gram is None else gram) + _dot_nt(tsib[rows, :], tsib[win, :])
             gp[q, :, 0:GW] = gram[:, 0:GW]
             last = gram[:, GW:PW]
             right = jnp.logical_and(c == 1, lax.broadcasted_iota(jnp.int32, (HR, BLK), 1) < HR)
             gp[q, 0:HR, GW:PW] = jnp.where(right, pltpu.roll(last[HR:], HR, 1), last[:HR])
             gp[q, HR:BLK, GW:PW] = zall[q] + zrcv[q]
 
+        panel(first_q, gp[first_q])
+
+        @pl.when(is_end)
+        def _():
+            for i in range(NCH):
+                chain_copy(i, e1).start()
+
         def mk_panels(m, cc):
-            k = jnp.where(is_end, jnp.where(m == 0, 2, jnp.where(m < 3, m - 1, 3)), m)
-            e = jnp.where(k % 2 == 0, e1, e2)
-            panel(jnp.where(k < 2, qf(1 - y, e), qz(1 - y, e)))
-
-            @pl.when(jnp.logical_and(k < 2, jnp.logical_or(is_mid, k == 0)))
+            e = jnp.where(m == 0, e1, e2)
+            panel(jnp.where(m < 2, qf(1 - y, e), qz(1 - y, e)))
+
+            @pl.when(jnp.logical_or(m == 0, jnp.logical_and(m == 1, is_mid)))
             def _():
                 for i in range(NCH):
                     fy_copy(e, i).start()
-
-            @pl.when(jnp.logical_and(is_end, m == 0))
-            def _():
-                for i in range(NCH):
-                    chain_copy(i, e1).start()
             return cc
 
-        lax.fori_loop(0, 4, mk_panels, 0)
+        lax.fori_loop(0, 3, mk_panels, 0)
 
         def late_panels(m, cc):
             e = jnp.where(m % 2 == 0, e1, e2)
@@ -438,17 +446,27 @@
             @pl.when(jnp.logical_and(m % KCH == KCH - 1, m >= KCH))
             def _():
                 from_sib(panel_q(m // KCH - 1, e1))
+
+            @pl.when(m == 2 * KCH)
+            def _():
+                from_y(e2)
+
+            @pl.when(m == 2 * KCH + 1)
+            def _():
+                from_y(e1)
+
+            @pl.when(m == 2 * KCH + 2)
+            def _():
+                from_sib(qf(1 - y, e2))
             return cc
 
         lax.fori_loop(0, 3 * KCH, k_round, 0)
-        from_y(e2)
-        from_y(e1)
 
         def last_sib(k, cc):
-            from_sib(jnp.where(k == 0, qf(1 - y, e2), jnp.where(k == 1, qf(1 - y, e1), jnp.where(k == 2, panel_q(2, e2), panel_q(2, e1)))))
+            from_sib(jnp.where(k == 0, qf(1 - y, e1), jnp.where(k == 1, panel_q(2, e2), panel_q(2, e1))))
             return cc
 
-        lax.fori_loop(0, 4, last_sib, 0)
+        lax.fori_loop(0, 3, last_sib, 0)
 
         for e in range(2):
             s_copy(1 - y, e, 2 + e).wait_send()
@@ -580,9 +598,9 @@
         body = lambda *refs: _kernel(n_total, kern_width, step_size, *refs)
         return pl.pallas_call(
             body,
-            out_shape=jax.ShapeDtypeStruct((rows_loc, feat_loc), F32),
+            out_shape=pltpu.VMEM((rows_loc, feat_loc), F32),
             in_specs=[anym, anym, anym, anym],
-            out_specs=anym,
+            out_specs=pl.BlockSpec(memory_space=pltpu.VMEM),
             scratch_shapes=[
                 pltpu.VMEM((n_total, width), F32),
                 pltpu.VMEM((2, n_total, width), BF),
@@ -605,7 +623,7 @@
                 dma((2, 3 * KCH)), dma((2, 3 * KCH)), dma((2, 2, KCH)), dma((2, 2, KCH)), dma((8, KCH)), dma((8, KCH)),
                 dma((8,)), dma((4, 2)),
             ],
-            compiler_params=pltpu.CompilerParams(collective_id=0, has_side_effects=True, vmem_limit_bytes=63 * 1024 * 1024),
+            compiler_params=pltpu.CompilerParams(collective_id=0, has_side_effects=True, vmem_limit_bytes=54 * 1024 * 1024),
             name="svgd",
         )(local_theta, prec_loc[None, :], mean_loc[None, :], factor_loc.T)
 

time: 553 us -> 545 us (0.986)
  no operation moved by 1% of the time
where the time goes in v5:
time: 545 us; the launch traced here: 544 us
  Pallas kernels  542 us (99%)
    pallas_call x1, Pallas kernels, local_steps(): pl.pallas_call(body, out_shape=pltpu.VMEM((rows_loc, feat_loc), F32), in_...  542 us

profile of v5, /device:TPU:0, one launch (start us, length us, event | category | flops | bytes accessed | tf_op | source)
XLA Modules:
  0.0 544.5 jit_solution(8754254296815106217)
XLA Ops:
  0.0 541.8 %svgd.1 = f32[512,3072]{1,0:T(8,128)S(1)} custom-call(f32[512,3072]{1,0:T(8,128)} %refs_0_.1, f32[1,3072]{1,0:T(1,128)} %bitcast.4, f32[1,3072]{1,0:T(1,128)} %bitcast.5, bf16[64,3072]{1,0:T(8,128)(2,1)} %bitcast.3), custom_call_target="tpu_custom_call" | custom-call | tf_op jit(solution)/shard_map/svgd/pallas_call | solution.py:599
  541.8 2.7 copy.6

commit v6 on v5

--- a/solution.py
+++ b/solution.py
@@ -17,7 +17,7 @@
 HR = BLK // 2
 FSTART = 4
 YFWD = (17, 20, 22, 23)
-SKEW = 3
+SKEW = 2
 TILE = 256
 BF = jnp.bfloat16
 F32 = jnp.float32
@@ -136,7 +136,8 @@
             zall[b] = jnp.where(low_lanes, z_blk[:HR], pltpu.roll(z_blk[HR:], HR, 1))
 
     def first_rows(k, carry):
-        zz = (z + k) % 4
+        partner = jnp.where(z < 2, 1 - z, 5 - z)
+        zz = jnp.where(k == 0, z, jnp.where(k == 1, partner, jnp.where(k == 2, (z + 2) % 4, (partner + 2) % 4)))
 
         @pl.when(k == 0)
         def _():
@@ -153,9 +154,6 @@
 
     lax.fori_loop(0, 4, first_rows, 0)
     z_copy().start()
-    for k in range(1, 4):
-        in_copy((z + k) % 4).wait_send()
-
     def qf(yy, e):
         return yy * 2 + e
 
@@ -559,6 +557,9 @@
         return carry
 
     lax.fori_loop(0, NUM_STEPS, step, 0)
+
+    for k in range(1, 4):
+        in_copy((z + k) % 4).wait_send()
 
     def out_wait(i, cc):
         zz = (i // 2 + 2 * c) % 4

time: 545 us -> 542 us (level)
  no operation moved by 1% of the time
where the time goes in v6:
time: 542 us; the launch traced here: 541 us
  Pallas kernels  539 us (99%)
    pallas_call x1, Pallas kernels, local_steps(): pl.pallas_call(body, out_shape=pltpu.VMEM((rows_loc, feat_loc), F32), in_...  539 us

profile of v6, /device:TPU:0, one launch (start us, length us, event | category | flops | bytes accessed | tf_op | source)
XLA Modules:
  0.0 541.5 jit_solution(16833115094959911983)
XLA Ops:
  0.0 538.7 %svgd.1 = f32[512,3072]{1,0:T(8,128)S(1)} custom-call(f32[512,3072]{1,0:T(8,128)} %refs_0_.1, f32[1,3072]{1,0:T(1,128)} %bitcast.4, f32[1,3072]{1,0:T(1,128)} %bitcast.5, bf16[64,3072]{1,0:T(8,128)(2,1)} %bitcast.3), custom_call_target="tpu_custom_call" | custom-call | tf_op jit(solution)/shard_map/svgd/pallas_call | solution.py:600
  538.7 2.7 copy.6
